TPU v7x, 1024 devices: a whole 4x4x32 slice. The times are simulated.
1024 devices in a mesh: gx: 64 (over z, core), gy: 16 (over x, y).
Axes of the slice: x: 4, y: 4, z: 32, core: 2. Of those that a mesh axis runs over, the one named last changes fastest.
Arguments:
- suction_potential: float32 [512, 128, 128], P('gx', 'gy'), may hold values from -3 to 0.3
- ground_warmth: float32 [512, 128, 128], P('gx', 'gy'), may hold values from -4 to 4
- ground_category: int32 [512, 128, 128], P('gx', 'gy'), may hold values from 0 to 11
- icebound_flag: int32 [512, 128, 128], P('gx', 'gy'), may hold values 0 or 1
- ground_wetted_permeability: float32 [12], replicated, may hold values from 0.02 to 0.15
- ground_falloff_exponent: float32 [12], replicated, may hold values from 0.3 to 1.5
- camera_skew_per_plane: float32 [4], replicated, may hold values from -1 to 1
- hue_gradient_steepness: float32 [3], replicated, may hold values from 4 to 16
- hue_gradient_middles: float32 [3], replicated, may hold values from 0.1 to 0.4
- camera_distance_ordering: int32 [4, 16], replicated, may hold values from 0 to 15, as said below
Outputs:
- head_out: float32 [512, 128, 128], P('gx', 'gy')
- temp_out: float32 [512, 128, 128], P('gx', 'gy')
- image: float32 [4, 4, 512, 128], P(None, None, 'gx', 'gy')
Inputs may be any that keep to these rules, and one draw needn't show every extreme that they name: Each row of camera_distance_ordering names every slab 0 to 15 once.
All inputs are finite; a program needn't handle non-finite values. No bound on the sum of `icebound_flag` on one device may be relied on, other than what follows from the above.
Results may differ from a plain program's by a relative error of at most 0.0003.
Values sent between devices are 32-bit elements; how exact they have to be, the bound alone decides.
A program may use at most 32 MiB of HBM per device.

v0:
```python
import jax
import jax.numpy as jnp
from jax import lax
from jax.sharding import PartitionSpec as P

STEPS = 2


IMPEDANCE = 4.0
DIFFUSE = 0.12


def with_halo(x, sides, width):
    for axis, dim in sides:
        count, length = (lax.axis_size(axis), x.shape[dim])
        up = [(i, (i + 1) % count) for i in range(count - 1)]
        down = [(j, i) for i, j in up]
        last = lax.slice_in_dim(x, length - width, length, axis=dim)
        first = lax.slice_in_dim(x, 0, width, axis=dim)
        before = lax.ppermute(last, axis, up)
        after = lax.ppermute(first, axis, down)
        x = jnp.concatenate([before, x, after], axis=dim)
    return x


def voxel_index_map(ground_category, table):
    total = jnp.zeros(ground_category.shape, jnp.float32)
    for number in range(table.shape[0]):
        total = total + jnp.where(ground_category == number, table[number], jnp.float32(0.0))
    return total


def advance(evolving_arrays, first_row, first_col, rows_all, cols_all):
    suction_potential, temp, conduct_sat, alpha, ice = evolving_arrays
    conduct = (
        conduct_sat
        * jnp.exp(alpha * jnp.minimum(suction_potential, 0.0))
        * jnp.exp(-IMPEDANCE * ice * jax.nn.sigmoid(-2.0 * temp))
    )
    global_rows = first_row + jnp.arange(suction_potential.shape[0], dtype=jnp.int32)
    global_cols = first_col + jnp.arange(suction_potential.shape[1], dtype=jnp.int32)
    open_rows = ((global_rows[:-1] >= 0) & (global_rows[1:] <= rows_all - 1))[:, None, None]
    open_cols = ((global_cols[:-1] >= 0) & (global_cols[1:] <= cols_all - 1))[None, :, None]
    flux_rows = jnp.where(
        open_rows,
        0.5 * (conduct[1:] + conduct[:-1]) * (suction_potential[1:] - suction_potential[:-1]),
        0.0,
    )
    flux_cols = jnp.where(
        open_cols,
        0.5
        * (conduct[:, 1:] + conduct[:, :-1])
        * (suction_potential[:, 1:] - suction_potential[:, :-1]),
        0.0,
    )
    flux_up = (
        0.5
        * (conduct[..., 1:] + conduct[..., :-1])
        * (suction_potential[..., 1:] - suction_potential[..., :-1] + 1.0)
    )
    zeros_up = jnp.zeros(suction_potential.shape[:2] + (1,), suction_potential.dtype)
    change_up = jnp.concatenate([flux_up, zeros_up], 2) - jnp.concatenate([zeros_up, flux_up], 2)
    change = (
        flux_rows[1:, 1:-1]
        - flux_rows[:-1, 1:-1]
        + (flux_cols[1:-1, 1:] - flux_cols[1:-1, :-1])
        + change_up[1:-1, 1:-1]
    )
    inside = ((global_rows[1:-1] >= 0) & (global_rows[1:-1] <= rows_all - 1))[:, None, None] & (
        (global_cols[1:-1] >= 0) & (global_cols[1:-1] <= cols_all - 1)
    )[None, :, None]
    head_new = jnp.where(inside, suction_potential[1:-1, 1:-1] + change, 0.0)
    vertical = jnp.concatenate([temp[..., 1:], zeros_up], 2) + jnp.concatenate(
        [zeros_up, temp[..., :-1]], 2
    )
    laplace = (
        temp[2:, 1:-1]
        + temp[:-2, 1:-1]
        + temp[1:-1, 2:]
        + temp[1:-1, :-2]
        + vertical[1:-1, 1:-1]
        - 6.0 * temp[1:-1, 1:-1]
    )
    temp_new = jnp.where(inside, temp[1:-1, 1:-1] + DIFFUSE * laplace, 0.0)
    return (head_new, temp_new, conduct_sat[1:-1, 1:-1], alpha[1:-1, 1:-1], ice[1:-1, 1:-1])


def moisture(suction_potential):
    return 0.05 + 0.4 * jnp.exp(0.8 * jnp.minimum(suction_potential, 0.0))


def render(theta, first_plane, planes_all, groups, tilt, gain, middle):
    depth_z = theta.shape[2]
    planes = first_plane + jnp.arange(theta.shape[1], dtype=jnp.int32)
    shift = tilt * (planes.astype(jnp.float32) - 0.5 * planes_all)
    wrapped = shift - depth_z * jnp.floor(shift / depth_z)
    base = jnp.floor(wrapped)
    frac = wrapped - base
    offset = base.astype(jnp.int32) % depth_z
    doubled = jnp.concatenate([theta, theta], 2)

    def plane_slices(column, start):
        lower_part = lax.dynamic_slice_in_dim(column, start, depth_z, 1)
        upper_part = lax.dynamic_slice_in_dim(column, start + 1, depth_z, 1)
        return (lower_part, upper_part)

    lower_vals, upper_vals = jax.vmap(plane_slices, in_axes=(1, 0), out_axes=(1, 1))(
        doubled, offset
    )
    sample = (1.0 - frac)[None, :, None] * lower_vals + frac[None, :, None] * upper_vals
    shape_four = (theta.shape[0], groups, theta.shape[1] // groups, depth_z)
    sample = sample.reshape(shape_four)
    optical = sample * (8.0 / planes_all)
    before = jnp.cumsum(optical, axis=2) - optical
    weight = (1.0 - jnp.exp(-optical)) * jnp.exp(-before)
    layers = [
        jnp.sum(jax.nn.sigmoid(gain[color] * (sample - middle[color])) * weight, axis=2)
        for color in range(3)
    ]
    layers.append(jnp.sum(optical, axis=2))
    return jnp.stack(layers, 0).transpose(2, 0, 1, 3)


def shards(
    suction_potential,
    ground_warmth,
    ground_category,
    icebound_flag,
    ground_wetted_permeability,
    ground_falloff_exponent,
    camera_skew_per_plane,
    hue_gradient_steepness,
    hue_gradient_middles,
    camera_distance_ordering,
):
    rows_dev = suction_potential.shape[0]
    cols_dev = suction_potential.shape[1]
    rows_all = rows_dev * lax.axis_size("gx")
    cols_all = cols_dev * lax.axis_size("gy")
    row_start = lax.axis_index("gx") * rows_dev
    col_start = lax.axis_index("gy") * cols_dev
    evolving_arrays = (
        suction_potential,
        ground_warmth,
        voxel_index_map(ground_category, ground_wetted_permeability),
        voxel_index_map(ground_category, ground_falloff_exponent),
        icebound_flag.astype(jnp.float32),
    )
    extended = with_halo(jnp.stack(evolving_arrays), (("gx", 1), ("gy", 2)), STEPS)
    evolving_arrays = tuple((extended[number] for number in range(5)))
    for number in range(STEPS):
        margin = STEPS - number
        evolving_arrays = advance(
            evolving_arrays, row_start - margin, col_start - margin, rows_all, cols_all
        )
    theta = moisture(evolving_arrays[0])

    def one_view(tilt):
        return render(
            theta, col_start, cols_all, 1, tilt, hue_gradient_steepness, hue_gradient_middles
        )[0]

    pieces = lax.map(one_view, camera_skew_per_plane)
    received = lax.all_to_all(pieces[None], "gy", split_axis=4, concat_axis=0, tiled=True)
    in_front = (camera_distance_ordering[:, None, :] < camera_distance_ordering[:, :, None]).astype(
        jnp.float32
    )
    depth = received[:, :, 3]
    front = jnp.einsum("vij,jvxz->ivxz", in_front, depth, precision=lax.Precision.HIGHEST)
    color = jnp.sum(jnp.exp(-front)[:, :, None] * received[:, :, :3], axis=0)
    opacity = 1.0 - jnp.exp(-jnp.sum(depth, axis=0))
    image = jnp.concatenate([color, opacity[:, None]], 1)
    return (evolving_arrays[0], evolving_arrays[1], image)


def solution(mesh):
    placed = (
        P("gx", "gy", None),
        P("gx", "gy", None),
        P("gx", "gy", None),
        P("gx", "gy", None),
        P(),
        P(),
        P(),
        P(),
        P(),
        P(),
    )
    return jax.shard_map(
        shards,
        mesh=mesh,
        in_specs=placed,
        out_specs=(P("gx", "gy", None), P("gx", "gy", None), P(None, None, "gx", "gy")),
        check_vma=False,
    )
```

profile of v0, /device:TPU:1, one launch (start us, length us, event | category | flops | bytes accessed | tf_op | source)
XLA Modules:
  0.0 103.6 jit_solution(16295088599964307849)
XLA Ops:
  0.6 1.8 %fusion.79 = (f32[1]{0:T(128)}, f32[1]{0:T(128)}, f32[1]{0:T(128)}, f32[1]{0:T(128)}, f32[1]{0:T(128)}, /*index=5*/f32[1]{0:T(128)}, f32[1]{0:T(128)}, f32[1]{0:...) fusion(f32[12]{0:T(128)} %param.16), kind=kLoop, calls=%fused_computation.171 | loop fusion | bytes 96 | tf_op jit(solution)/shard_map/slice | solution.py:29
  2.4 0.8 bitcast_dynamic-update-slice_fusion.4
  3.2 0.7 fusion.78
  3.9 0.7 copy-done.5
  4.7 7.6 %bitcast_dynamic-update-slice_fusion.2 = (f32[5,8,8,128]{3,2,1,0:T(8,128)S(1)}, pred[8,8,128]{2,1,0:T(8,128)(4,1)S(1)}, pred[8,8,128]{2,1,0:T(8,128)(4,1)S(1)}, ...) fusion(f32[5,8,8,128]{3,2,1,0:T(8,128)S(1)} %bitcast_dynamic-up, ...), kind=kLoop, calls=%fused_computation.130 | loop fusion | flops 286720 | bytes 163888
  12.3 7.6 %bitcast_dynamic-update-slice_fusion.1 = f32[5,8,8,128]{3,2,1,0:T(8,128)S(1)} fusion(f32[5,8,8,128]{3,2,1,0:T(8,128)S(1)} %get-tuple-element.167, pred[8,8,128]{2,1,0:T(8,128)(4,1)S(1)} %get-tuple-element.179, pred[8,8,128]{2,1,0:T(8,128)(4,1)S(1)} %get-tuple-element.178, pred[8,8,128]{2,1,0:T(8,128)(4,1)S(1)} %get-tuple-element.177, ...), kind=kLoop, calls=%fused_computation.129 | loop fusion | flops 188416 | bytes 131120
  19.9 4.9 %collective-permute-start = (f32[5,2,8,128]{3,2,1,0:T(8,128)S(1)}, f32[5,2,8,128]{3,2,1,0:T(8,128)S(1)}, u32[]{:S(2)}, u32[]{:S(2)}) collective-permute-start(f32[5,2,8,128]{3,2,1,0:T(8,128)S(1)} %get-tuple-element.198), channel_id=1, source_target_pairs={{0,16},{16,32},{32,48},{48,64},{64,80},{80,96},{96,112},{112,128},... | collective-permute-start | bytes 122888 | tf_op jit(solution)/shard_map/ppermute | solution.py:20
  24.9 12.4 %collective-permute-start.1 = (f32[5,2,8,128]{3,2,1,0:T(8,128)S(1)}, f32[5,2,8,128]{3,2,1,0:T(8,128)S(1)}, u32[]{:S(2)}, u32[]{:S(2)}) collective-permute-start(f32[5,2,8,128]{3,2,1,0:T(8,128)S(1)} %get-tuple-element.199), channel_id=1, source_target_pairs={{16,0},{32,16},{48,32},{64,48},{80,64},{96,80},{112,96},{128,112},... | collective-permute-start | bytes 122888 | tf_op jit(solution)/shard_map/ppermute | solution.py:21
  38.2 1.3 %collective-permute-start.2 = (f32[5,12,2,128]{3,2,1,0:T(2,128)S(1)}, f32[5,12,2,128]{3,2,1,0:T(2,128)S(1)}, u32[]{:S(2)}, u32[]{:S(2)}) collective-permute-start(f32[5,12,2,128]{3,2,1,0:T(2,128)S(1)} %get-tuple-element.196), channel_id=1, source_target_pairs={{0,1},{1,2},{2,3},{3,4},{4,5},{5,6},{6,7},{7,8},{8,9},{9,10},{10,1... | collective-permute-start | bytes 184328 | tf_op jit(solution)/shard_map/ppermute | solution.py:20
  39.5 1.3 %collective-permute-start.3 = (f32[5,12,2,128]{3,2,1,0:T(2,128)S(1)}, f32[5,12,2,128]{3,2,1,0:T(2,128)S(1)}, u32[]{:S(2)}, u32[]{:S(2)}) collective-permute-start(f32[5,12,2,128]{3,2,1,0:T(2,128)S(1)} %get-tuple-element.197), channel_id=1, source_target_pairs={{1,0},{2,1},{3,2},{4,3},{5,4},{6,5},{7,6},{8,7},{9,8},{10,9},{11,1... | collective-permute-start | bytes 184328 | tf_op jit(solution)/shard_map/ppermute | solution.py:21
  40.8 3.6 %collective-permute-done.3 = f32[5,12,2,128]{3,2,1,0:T(2,128)S(1)} collective-permute-done((f32[5,12,2,128]{3,2,1,0:T(2,128)S(1)}, f32[5,12,2,128]{3,2,1,0:T(2,128)S(1)}, u32[]{:S(2)}, u32[]{:S(2)}) %collective-permute-start.3) | collective-permute-done | bytes 61472 | tf_op jit(solution)/shard_map/ppermute | solution.py:21
  45.6 0.7 multiply_add_fusion.1
  47.0 40.9 %while.12 = (s32[]{:T(128)}, f32[4,4,8,128]{3,2,1,0:T(8,128)S(1)}, f32[3]{0:T(128)S(1)}, f32[4]{0:T(128)S(1)}, s32[]{:T(128)}, /*index=5*/f32[8,8,256]{0,1,2:T(8,128)S(1)}, f32[3]{0:T(128)S(1)}, s32[]{:T(128)}) while((s32[]{:T(128)}, f32[4,4,8,128]{3,2,1,0:T(8,128)S(1)}, f32[3]{0:T(128)S(1)}, f32[4]{0:T(128)S(1)}, s32[]{:T(128)}, ...), condition=%wide.region_6.7_spmd, body=%wide.region_0.6_spmd.sunk | while | flops 352634 | bytes 442941 | solution.py:163
  47.0 0.6 dynamic_slice.8
  47.6 0.6 or_bitcast_fusion.2
  48.3 1.3 %gather_fusion = f32[8,8,128]{1,0,2:T(8,128)S(1)} fusion(f32[8,8,256]{1,0,2:T(8,128)S(1)} %bitcast.158, s32[8]{0:T(128)S(1)} %get-tuple-element.297), kind=kCustom, calls=%fused_computation.1.clone.1 | custom fusion | bytes 65632 | tf_op jit(solution)/shard_map/while/body/eval_jaxpr/vmap()/gather | solution.py:104
  49.8 1.3 %gather_fusion.1 = f32[8,8,128]{1,0,2:T(8,128)S(1)} fusion(f32[8,8,256]{1,0,2:T(8,128)S(1)} %bitcast.159, s32[8]{0:T(128)S(1)} %get-tuple-element.299), kind=kCustom, calls=%fused_computation.clone.1 | custom fusion | bytes 65632 | tf_op jit(solution)/shard_map/while/body/eval_jaxpr/vmap()/gather | solution.py:103
  51.3 0.7 fusion.83
  52.0 0.6 broadcast_subtract_fusion.2
  52.6 3.9 %fusion.84 = (f32[8,128]{1,0:T(8,128)S(1)}, f32[8,128]{1,0:T(8,128)S(1)}, f32[8,128]{1,0:T(8,128)S(1)}, f32[8,128]{1,0:T(8,128)S(1)}) fusion(f32[]{:T(128)} %bitcast.146, f32[]{:T(128)} %bitcast.147, f32[]{:T(128)} %bitcast.148, f32[]{:T(128)} %bitcast.149, f32[]{:T(128)} %bitcast.150, f32[]{:T(128)} %bitcast.151, f32[8,8,128]{2,1,0:T(8,128)S(1)} %copy.75, ...), kind=kOutput, calls=%fused_computation.16.clone.1 | output fusion | flops 339968 | bytes 82008 | tf_op jit(solution)/shard_map/while/body/eval_jaxpr/jit(cumsum)/reduce_window_sum | solution.py:114
  57.2 0.7 dynamic_slice.8
  57.9 0.6 or_bitcast_fusion.2
  58.5 1.3 %gather_fusion = f32[8,8,128]{1,0,2:T(8,128)S(1)} fusion(f32[8,8,256]{1,0,2:T(8,128)S(1)} %bitcast.158, s32[8]{0:T(128)S(1)} %get-tuple-element.297), kind=kCustom, calls=%fused_computation.1.clone.1 | custom fusion | bytes 65632 | tf_op jit(solution)/shard_map/while/body/eval_jaxpr/vmap()/gather | solution.py:104
  60.0 1.3 %gather_fusion.1 = f32[8,8,128]{1,0,2:T(8,128)S(1)} fusion(f32[8,8,256]{1,0,2:T(8,128)S(1)} %bitcast.159, s32[8]{0:T(128)S(1)} %get-tuple-element.299), kind=kCustom, calls=%fused_computation.clone.1 | custom fusion | bytes 65632 | tf_op jit(solution)/shard_map/while/body/eval_jaxpr/vmap()/gather | solution.py:103
  61.5 0.7 fusion.83
  62.2 0.6 broadcast_subtract_fusion.2
  62.9 3.9 %fusion.84 = (f32[8,128]{1,0:T(8,128)S(1)}, f32[8,128]{1,0:T(8,128)S(1)}, f32[8,128]{1,0:T(8,128)S(1)}, f32[8,128]{1,0:T(8,128)S(1)}) fusion(f32[]{:T(128)} %bitcast.146, f32[]{:T(128)} %bitcast.147, f32[]{:T(128)} %bitcast.148, f32[]{:T(128)} %bitcast.149, f32[]{:T(128)} %bitcast.150, f32[]{:T(128)} %bitcast.151, f32[8,8,128]{2,1,0:T(8,128)S(1)} %copy.75, ...), kind=kOutput, calls=%fused_computation.16.clone.1 | output fusion | flops 339968 | bytes 82008 | tf_op jit(solution)/shard_map/while/body/eval_jaxpr/jit(cumsum)/reduce_window_sum | solution.py:114
  67.4 0.7 dynamic_slice.8
  68.1 0.6 or_bitcast_fusion.2
  68.7 1.3 %gather_fusion = f32[8,8,128]{1,0,2:T(8,128)S(1)} fusion(f32[8,8,256]{1,0,2:T(8,128)S(1)} %bitcast.158, s32[8]{0:T(128)S(1)} %get-tuple-element.297), kind=kCustom, calls=%fused_computation.1.clone.1 | custom fusion | bytes 65632 | tf_op jit(solution)/shard_map/while/body/eval_jaxpr/vmap()/gather | solution.py:104
  70.2 1.3 %gather_fusion.1 = f32[8,8,128]{1,0,2:T(8,128)S(1)} fusion(f32[8,8,256]{1,0,2:T(8,128)S(1)} %bitcast.159, s32[8]{0:T(128)S(1)} %get-tuple-element.299), kind=kCustom, calls=%fused_computation.clone.1 | custom fusion | bytes 65632 | tf_op jit(solution)/shard_map/while/body/eval_jaxpr/vmap()/gather | solution.py:103
  71.8 0.7 fusion.83
  72.5 0.6 broadcast_subtract_fusion.2
  73.1 3.9 %fusion.84 = (f32[8,128]{1,0:T(8,128)S(1)}, f32[8,128]{1,0:T(8,128)S(1)}, f32[8,128]{1,0:T(8,128)S(1)}, f32[8,128]{1,0:T(8,128)S(1)}) fusion(f32[]{:T(128)} %bitcast.146, f32[]{:T(128)} %bitcast.147, f32[]{:T(128)} %bitcast.148, f32[]{:T(128)} %bitcast.149, f32[]{:T(128)} %bitcast.150, f32[]{:T(128)} %bitcast.151, f32[8,8,128]{2,1,0:T(8,128)S(1)} %copy.75, ...), kind=kOutput, calls=%fused_computation.16.clone.1 | output fusion | flops 339968 | bytes 82008 | tf_op jit(solution)/shard_map/while/body/eval_jaxpr/jit(cumsum)/reduce_window_sum | solution.py:114
  77.6 0.7 dynamic_slice.8
  78.3 0.6 or_bitcast_fusion.2
  79.0 1.3 %gather_fusion = f32[8,8,128]{1,0,2:T(8,128)S(1)} fusion(f32[8,8,256]{1,0,2:T(8,128)S(1)} %bitcast.158, s32[8]{0:T(128)S(1)} %get-tuple-element.297), kind=kCustom, calls=%fused_computation.1.clone.1 | custom fusion | bytes 65632 | tf_op jit(solution)/shard_map/while/body/eval_jaxpr/vmap()/gather | solution.py:104
  80.5 1.3 %gather_fusion.1 = f32[8,8,128]{1,0,2:T(8,128)S(1)} fusion(f32[8,8,256]{1,0,2:T(8,128)S(1)} %bitcast.159, s32[8]{0:T(128)S(1)} %get-tuple-element.299), kind=kCustom, calls=%fused_computation.clone.1 | custom fusion | bytes 65632 | tf_op jit(solution)/shard_map/while/body/eval_jaxpr/vmap()/gather | solution.py:103
  82.0 0.7 fusion.83
  82.7 0.6 broadcast_subtract_fusion.2
  83.3 3.9 %fusion.84 = (f32[8,128]{1,0:T(8,128)S(1)}, f32[8,128]{1,0:T(8,128)S(1)}, f32[8,128]{1,0:T(8,128)S(1)}, f32[8,128]{1,0:T(8,128)S(1)}) fusion(f32[]{:T(128)} %bitcast.146, f32[]{:T(128)} %bitcast.147, f32[]{:T(128)} %bitcast.148, f32[]{:T(128)} %bitcast.149, f32[]{:T(128)} %bitcast.150, f32[]{:T(128)} %bitcast.151, f32[8,8,128]{2,1,0:T(8,128)S(1)} %copy.75, ...), kind=kOutput, calls=%fused_computation.16.clone.1 | output fusion | flops 339968 | bytes 82008 | tf_op jit(solution)/shard_map/while/body/eval_jaxpr/jit(cumsum)/reduce_window_sum | solution.py:114
  87.9 0.6 copy.54
  88.6 1.1 %reshape.252 = f32[16,1,1024]{2,1,0:T(1,128)S(1)} reshape(f32[128,1,4,4,8]{4,3,2,1,0:T(4,128)S(1)} %bitcast_bitcast_fusion) | data formatting | bytes 131072
  89.7 9.1 %all_to_all.18 = f32[16,1,1024]{2,1,0:T(1,128)S(1)} all-to-all(f32[16,1,1024]{2,1,0:T(1,128)S(1)} %reshape.252), channel_id=1, replica_groups=mesh['gx'=64,'gy'=16] {'gy'}, dimensions={0} | all-to-all | bytes 131072 | tf_op jit(solution)/shard_map/all_to_all | solution.py:164
  99.3 0.8 reduce.21
  100.1 1.2 %reshape.253 = f32[128,1,4,4,8]{4,3,2,1,0:T(4,128)S(1)} reshape(f32[16,1024]{1,0:T(8,128)S(1)} %reduce.21) | data formatting | bytes 131072
  101.4 1.0 copy.56
  102.9 0.6 copy.57
  (99 shorter events, 7.9 us)
Async XLA Ops:
  2.4 0.8 copy-start.2
  2.4 1.5 %copy-start.3 = (f32[8,8,128]{2,1,0:T(8,128)S(1)}, f32[8,8,128]{2,1,0:T(8,128)}, u32[]{:S(2)}) copy-start(f32[8,8,128]{2,1,0:T(8,128)} %param.13) | copy-start | bytes 98308
  3.9 0.8 copy-start.5
  12.3 7.6 %copy-start.4 = (s32[8,8,128]{2,1,0:T(8,128)S(1)}, s32[8,8,128]{2,1,0:T(8,128)}, u32[]{:S(2)}) copy-start(s32[8,8,128]{2,1,0:T(8,128)} %param.15) | copy-start | bytes 98308
  19.9 17.9 %collective-permute-start = (f32[5,2,8,128]{3,2,1,0:T(8,128)S(1)}, f32[5,2,8,128]{3,2,1,0:T(8,128)S(1)}, u32[]{:S(2)}, u32[]{:S(2)}) collective-permute-start(f32[5,2,8,128]{3,2,1,0:T(8,128)S(1)} %get-tuple-element.198), channel_id=1, source_target_pairs={{0,16},{16,32},{32,48},{48,64},{64,80},{80,96},{96,112},{112,128},... | collective-permute-start | bytes 122888 | tf_op jit(solution)/shard_map/ppermute | solution.py:20
  24.9 13.2 %collective-permute-start.1 = (f32[5,2,8,128]{3,2,1,0:T(8,128)S(1)}, f32[5,2,8,128]{3,2,1,0:T(8,128)S(1)}, u32[]{:S(2)}, u32[]{:S(2)}) collective-permute-start(f32[5,2,8,128]{3,2,1,0:T(8,128)S(1)} %get-tuple-element.199), channel_id=1, source_target_pairs={{16,0},{32,16},{48,32},{64,48},{80,64},{96,80},{112,96},{128,112},... | collective-permute-start | bytes 122888 | tf_op jit(solution)/shard_map/ppermute | solution.py:21
  38.2 2.7 %collective-permute-start.2 = (f32[5,12,2,128]{3,2,1,0:T(2,128)S(1)}, f32[5,12,2,128]{3,2,1,0:T(2,128)S(1)}, u32[]{:S(2)}, u32[]{:S(2)}) collective-permute-start(f32[5,12,2,128]{3,2,1,0:T(2,128)S(1)} %get-tuple-element.196), channel_id=1, source_target_pairs={{0,1},{1,2},{2,3},{3,4},{4,5},{5,6},{6,7},{7,8},{8,9},{9,10},{10,1... | collective-permute-start | bytes 184328 | tf_op jit(solution)/shard_map/ppermute | solution.py:20
  39.5 5.0 %collective-permute-start.3 = (f32[5,12,2,128]{3,2,1,0:T(2,128)S(1)}, f32[5,12,2,128]{3,2,1,0:T(2,128)S(1)}, u32[]{:S(2)}, u32[]{:S(2)}) collective-permute-start(f32[5,12,2,128]{3,2,1,0:T(2,128)S(1)} %get-tuple-element.197), channel_id=1, source_target_pairs={{1,0},{2,1},{3,2},{4,3},{5,4},{6,5},{7,6},{8,7},{9,8},{10,9},{11,1... | collective-permute-start | bytes 184328 | tf_op jit(solution)/shard_map/ppermute | solution.py:21
  46.3 0.7 copy-start
  46.3 0.7 copy-start.1
  46.3 0.7 copy-start.7
  101.4 1.1 %copy-start.6 = (s32[4,16]{1,0:T(4,128)S(1)}, s32[4,16]{1,0:T(4,128)}, u32[]{:S(2)}) copy-start(s32[4,16]{1,0:T(4,128)} %param.21) | copy-start | bytes 772
where the time goes:
time: 105 us; the launch traced here: 104 us
  other arithmetic  39.3 us (37%)
  local copies, waits for them, and re-layouts  30 us (29%)
  starting transfers between devices  19.9 us (19%)
  blocking collectives  9.07 us (9%)
  waiting for transfers between devices  3.87 us (4%)
    another operation x4, other arithmetic, render(): before = jnp.cumsum(optical, axis=2) - optical  15.5 us
    unnamed x2, other arithmetic  15.2 us
    ppermute x2, starting transfers between devices, with_halo(): after = lax.ppermute(first, axis, down)  13.7 us
    all_to_all x1, blocking collectives, shards(): lax.all_to_all(pieces[None], 'gy', split_axis=4, concat_axis=0, tiled=True)  9.07 us
    ppermute x2, starting transfers between devices, with_halo(): before = lax.ppermute(last, axis, up)  6.22 us
    gather x8, local copies, waits for them, and re-layouts, plane_slices(): lower_part = lax.dynamic_slice_in_dim(column, start, depth_z, 1)  6.08 us
    gather x8, local copies, waits for them, and re-layouts, plane_slices(): upper_part = lax.dynamic_slice_in_dim(column, start + 1, depth_z, 1)  6 us
    unnamed x22, local copies, waits for them, and re-layouts  4.87 us
  transfers between devices with their start and end apart: 4, of which 2 were waited for; matrix products, arithmetic and copies ran while one was open for 1% of the time, Pallas kernels for 0%

commit v1 on v0

v1 whole, which is shorter than its diff:
```python
import functools

import jax
import jax.numpy as jnp
from jax import lax
from jax.experimental import pallas as pl
from jax.experimental.pallas import tpu as pltpu
from jax.sharding import PartitionSpec as P

MESH = pl.DeviceIdType.MESH
SOILS = 12
VIEWS = 4
SIDE = 8
DEPTH = 128
GROUPS = 16
DIFFUSE = 0.12
F32 = jnp.float32


def lookup(category, table):
    total = jnp.full(category.shape, table[0], F32)
    for number in range(1, SOILS):
        total = jnp.where(category == number, table[number], total)
    return total


def conductivity(head, temp, ks, alpha, ice):
    return ks * jnp.exp(alpha * jnp.minimum(head, 0.0) + 2.0 * ice * (jnp.tanh(temp) - 1.0))


def vertical(head, temp, conduct, lane):
    above = pltpu.roll(head, DEPTH - 1, 1)
    conduct_above = pltpu.roll(conduct, DEPTH - 1, 1)
    flux = jnp.where(lane < DEPTH - 1, (conduct + conduct_above) * (above - head + 1.0), 0.0)
    change = flux - pltpu.roll(flux, 1, 1)
    warm = jnp.where(lane < DEPTH - 1, pltpu.roll(temp, DEPTH - 1, 1), 0.0) + jnp.where(
        lane > 0, pltpu.roll(temp, 1, 1), 0.0
    )
    return change, warm


def kernel(
    gx_count,
    gy_count,
    head_in,
    temp_in,
    cat_in,
    ice_in,
    ks_in,
    alpha_in,
    skew_in,
    steep_in,
    mid_in,
    order_in,
    head_out,
    temp_out,
    image_out,
    head_a,
    temp_a,
    cat_a,
    ice_a,
    ks_s,
    alpha_s,
    skew_s,
    steep_s,
    mid_s,
    order_s,
    y_send,
    y_recv,
    x_send,
    x_recv,
    c_send,
    c_recv,
    ghost,
    head_v,
    temp_v,
    piece_send,
    piece_recv,
    image_v,
    in_sem,
    par_sem,
    halo_send_sem,
    halo_recv_sem,
    piece_send_sem,
    piece_recv_sem,
    out_sem,
):
    gx, gy = lax.axis_index("gx"), lax.axis_index("gy")
    gx_lo, gx_hi = lax.rem(gx + gx_count - 1, gx_count), lax.rem(gx + 1, gx_count)
    gy_lo, gy_hi = lax.rem(gy + gy_count - 1, gy_count), lax.rem(gy + 1, gy_count)

    loads = [
        pltpu.make_async_copy(src, dst, in_sem.at[number])
        for number, (src, dst) in enumerate(
            ((head_in, head_a), (temp_in, temp_a), (cat_in, cat_a), (ice_in, ice_a))
        )
    ]
    params = [
        pltpu.make_async_copy(src, dst, par_sem.at[number])
        for number, (src, dst) in enumerate(
            (
                (ks_in, ks_s),
                (alpha_in, alpha_s),
                (skew_in, skew_s),
                (steep_in, steep_s),
                (mid_in, mid_s),
                (order_in, order_s),
            )
        )
    ]
    for copy in params[:2] + loads + params[2:]:
        copy.start()

    px, py = lax.div(gy, 4), lax.rem(gy, 4)
    shifts = sorted(
        ((dx, dy) for dx in range(4) for dy in range(4) if (dx, dy) != (0, 0)),
        key=lambda d: -(min(d[0], 4 - d[0]) + min(d[1], 4 - d[1])),
    )
    peers = [lax.rem(px + dx, 4) * 4 + lax.rem(py + dy, 4) for dx, dy in shifts]
    corners = ((gx_lo, gy_lo), (gx_lo, gy_hi), (gx_hi, gy_lo), (gx_hi, gy_hi))

    barrier = pltpu.get_barrier_semaphore()
    greeted = [(gx, peer) for peer in peers] + [*corners, (gx_lo, gy), (gx_hi, gy)]
    for device in greeted:
        pl.semaphore_signal(barrier, inc=1, device_id=device, device_id_type=MESH)

    row = lax.broadcasted_iota(jnp.int32, (SIDE, DEPTH), 0)
    lane = lax.broadcasted_iota(jnp.int32, (SIDE, DEPTH), 1)
    first, last = row == 0, row == SIDE - 1

    for copy in params[:2]:
        copy.wait()
    for copy in loads:
        copy.wait()

    def across(ref, y):
        return ref[pl.ds(y, SIDE, stride=SIDE), :]

    def tile(ref, x):
        return ref[pl.ds(x * SIDE, SIDE), :]

    head = [across(head_a, y) for y in range(SIDE)]
    temp = [across(temp_a, y) for y in range(SIDE)]
    category = [across(cat_a, y) for y in range(SIDE)]
    ice = [across(ice_a, y).astype(F32) for y in range(SIDE)]
    ks = [lookup(category[y], ks_s) for y in range(SIDE)]
    alpha = [lookup(category[y], alpha_s) for y in range(SIDE)]
    conduct = [
        conductivity(head[y], temp[y], ks[y], alpha[y], ice[y]) for y in range(SIDE)
    ]
    edge = {}
    for x in (0, 1, SIDE - 2, SIDE - 1):
        h, t, c = tile(head_a, x), tile(temp_a, x), tile(cat_a, x)
        i = tile(ice_a, x).astype(F32)
        k = conductivity(h, t, lookup(c, ks_s), lookup(c, alpha_s), i)
        edge[x] = (h, t, c.astype(F32), i, k)

    for side, (near, far) in enumerate(((0, 1), (SIDE - 1, SIDE - 2))):
        parts = (
            head[near],
            temp[near],
            category[near].astype(F32),
            ice[near],
            head[far],
            temp[far],
            conduct[far],
        )
        for number, part in enumerate(parts):
            y_send[side, pl.ds(number * SIDE, SIDE), :] = part
        parts = (*edge[near][:4], edge[far][0], edge[far][1], edge[far][4])
        for number, part in enumerate(parts):
            x_send[side, pl.ds(number * SIDE, SIDE), :] = part
    for number, (x, y) in enumerate(((0, 0), (0, 7), (7, 0), (7, 7))):
        for field, part in enumerate((head[y], temp[y], conduct[y], conduct[y])):
            c_send[number, pl.ds(field, 1), :] = part[x : x + 1, :]

    pl.semaphore_wait(barrier, len(greeted))

    def remote(src, dst, number, device):
        return pltpu.make_async_remote_copy(
            src_ref=src,
            dst_ref=dst,
            send_sem=halo_send_sem.at[number],
            recv_sem=halo_recv_sem.at[number],
            device_id=device,
            device_id_type=MESH,
        )

    for number, device in enumerate(corners):
        remote(c_send.at[number], c_recv.at[3 - number], 0, device).start()
    remote(y_send.at[0], y_recv.at[1], 1, (gx, gy_lo)).start()
    remote(y_send.at[1], y_recv.at[0], 1, (gx, gy_hi)).start()
    remote(x_send.at[0], x_recv.at[1], 2, (gx_lo, gy)).start()
    remote(x_send.at[1], x_recv.at[0], 2, (gx_hi, gy)).start()

    for copy in params[2:]:
        copy.wait()

    has_x = (gx > 0, gx < gx_count - 1)
    has_y = (gy > 0, gy < gy_count - 1)
    x_open = (jnp.logical_or(row > 0, has_x[0]), jnp.logical_or(row < SIDE - 1, has_x[1]))
    y_open = (jnp.logical_or(row > 0, has_y[0]), jnp.logical_or(row < SIDE - 1, has_y[1]))

    own_vertical = [vertical(head[y], temp[y], conduct[y], lane) for y in range(SIDE)]

    whole = (
        remote(c_send, c_recv, 0, (gx, gy_lo)),
        remote(y_send, y_recv, 1, (gx, gy_lo)),
        remote(x_send, x_recv, 2, (gx, gy_lo)),
    )
    for copy in whole:
        copy.wait_recv()

    def along_rows(value, before, after):
        return (
            jnp.where(first, before, pltpu.roll(value, 1, 0)),
            jnp.where(last, after, pltpu.roll(value, SIDE - 1, 0)),
        )

    def change_rows(head_, conduct_, temp_, ends, opened):
        (h_lo, t_lo, k_lo), (h_hi, t_hi, k_hi) = ends
        heads = along_rows(head_, h_lo, h_hi)
        temps = along_rows(temp_, t_lo, t_hi)
        conducts = along_rows(conduct_, k_lo, k_hi)
        total = sum(
            jnp.where(opened[s], (conduct_ + conducts[s]) * (heads[s] - head_), 0.0)
            for s in range(2)
        )
        return total, temps[0] + temps[1]

    def y_part(side, number):
        return y_recv[side, pl.ds(number * SIDE, SIDE), :]

    def x_part(side, number):
        return x_recv[side, pl.ds(number * SIDE, SIDE), :]

    def warm_if(present, value):
        return jnp.where(present, value, 0.0)

    def corner(xs, ys):
        number = 2 * xs + ys
        return (
            c_recv[number, pl.ds(0, 1), :],
            warm_if(jnp.logical_and(has_x[xs], has_y[ys]), c_recv[number, pl.ds(1, 1), :]),
            c_recv[number, pl.ds(2, 1), :],
        )

    y_ghost, x_ghost = [], []
    for part_of, present, dest in ((y_part, has_y, y_ghost), (x_part, has_x, x_ghost)):
        for side in range(2):
            h, t, c, i = (part_of(side, number) for number in range(4))
            k_s, a = lookup(c, ks_s), lookup(c, alpha_s)
            k = conductivity(h, t, k_s, a, i)
            far = tuple(part_of(side, number) for number in range(4, 7))
            dest.append((h, warm_if(present[side], t), k, k_s, a, i, far))

    for side in range(2):
        for field in range(3):
            ghost[side, field] = x_ghost[side][field]

    def step(h, t, change, warm):
        return h + 0.5 * change, t + DIFFUSE * (warm - 6.0 * t)

    def face(k_a, h_a, k_b, h_b):
        return (k_a + k_b) * (h_b - h_a)

    def ghost_step(cell, inner, ends, opened, present):
        h, t, k, k_s, a, i, far = cell
        change, warm = vertical(h, t, k, lane)
        rows, rows_warm = change_rows(h, k, t, ends, opened)
        change = change + rows + face(k, h, far[2], far[0]) + face(k, h, inner[2], inner[0])
        warm = warm + rows_warm + far[1] + inner[1]
        h, t = step(h, t, change, warm)
        return h, warm_if(present, t), conductivity(h, t, k_s, a, i)

    y_next = [
        ghost_step(
            y_ghost[side],
            (head[y], temp[y], conduct[y]),
            (corner(0, side), corner(1, side)),
            x_open,
            has_y[side],
        )
        for side, y in ((0, 0), (1, SIDE - 1))
    ]
    x_next = [
        ghost_step(
            x_ghost[side],
            (edge[x][0], edge[x][1], edge[x][4]),
            (corner(side, 0), corner(side, 1)),
            y_open,
            has_x[side],
        )
        for side, x in ((0, 0), (1, SIDE - 1))
    ]
    for side in range(2):
        for field in range(3):
            ghost[2 + side, field] = x_next[side][field]

    def main_step(head_, temp_, conduct_, lows, highs, slot, verticals):
        hs = [lows[0], *head_, highs[0]]
        ts = [lows[1], *temp_, highs[1]]
        ks_ = [lows[2], *conduct_, highs[2]]
        faces = [face(ks_[y], hs[y], ks_[y + 1], hs[y + 1]) for y in range(SIDE + 1)]
        faces[0] = jnp.where(has_y[0], faces[0], 0.0)
        faces[SIDE] = jnp.where(has_y[1], faces[SIDE], 0.0)
        result = []
        for y in range(SIDE):
            ends = tuple(
                tuple(ghost[slot + side, field, pl.ds(y, 1), :] for field in range(3))
                for side in range(2)
            )
            rows, rows_warm = change_rows(head_[y], conduct_[y], temp_[y], ends, x_open)
            change, warm = verticals[y]
            change = change + rows + faces[y + 1] - faces[y]
            warm = warm + rows_warm + ts[y] + ts[y + 2]
            result.append(step(head_[y], temp_[y], change, warm))
        return [r[0] for r in result], [r[1] for r in result]

    head, temp = main_step(head, temp, conduct, y_ghost[0], y_ghost[1], 0, own_vertical)
    conduct = [
        conductivity(head[y], temp[y], ks[y], alpha[y], ice[y]) for y in range(SIDE)
    ]
    verticals = [vertical(head[y], temp[y], conduct[y], lane) for y in range(SIDE)]
    head, temp = main_step(head, temp, conduct, y_next[0], y_next[1], 2, verticals)

    for y in range(SIDE):
        head_v[pl.ds(y, SIDE, stride=SIDE), :] = head[y]
        temp_v[pl.ds(y, SIDE, stride=SIDE), :] = temp[y]
    stores = [
        pltpu.make_async_copy(head_v, head_out, out_sem.at[0]),
        pltpu.make_async_copy(temp_v, temp_out, out_sem.at[1]),
    ]
    for copy in stores:
        copy.start()

    theta = [0.05 + 0.4 * jnp.exp(0.8 * jnp.minimum(h, 0.0)) for h in head]
    planes_all = gy_count * SIDE
    layers = []
    for view in range(VIEWS):
        clear = None
        sums = [None] * 3
        depth = None
        for y in range(SIDE):
            shift = skew_s[view] * ((gy * SIDE + y).astype(F32) - 0.5 * planes_all)
            wrapped = shift - DEPTH * jnp.floor(shift * (1.0 / DEPTH))
            base = jnp.floor(wrapped)
            part = wrapped - base
            turn = lax.rem(2 * DEPTH - base.astype(jnp.int32), DEPTH)
            lower = pltpu.roll(theta[y], turn, 1)
            upper = pltpu.roll(lower, DEPTH - 1, 1)
            sample = (1.0 - part) * lower + part * upper
            optical = sample * (8.0 / planes_all)
            passed = jnp.exp(-optical)
            after = passed if clear is None else clear * passed
            weight = (1.0 if clear is None else clear) - after
            clear = after
            depth = optical if depth is None else depth + optical
            for color in range(3):
                term = weight * jnp.tanh((0.5 * steep_s[color]) * (sample - mid_s[color]))
                sums[color] = term if sums[color] is None else sums[color] + term
        layers += [0.5 * ((1.0 - clear) + total) for total in sums]
        layers.append(depth)
    piece_send[...] = jnp.transpose(jnp.concatenate(layers, 0))

    def exchange(src, dst, device):
        return pltpu.make_async_remote_copy(
            src_ref=src,
            dst_ref=dst,
            send_sem=piece_send_sem,
            recv_sem=piece_recv_sem,
            device_id=device,
            device_id_type=MESH,
        )

    for peer in peers:
        exchange(
            piece_send.at[pl.ds(pl.multiple_of(peer * SIDE, SIDE), SIDE)],
            piece_recv.at[gy],
            (gx, peer),
        ).start()
    piece_recv[gy] = piece_send[pl.ds(pl.multiple_of(gy * SIDE, SIDE), SIDE), :]

    view_of = lax.div(lane, 4 * SIDE)
    kind_of = lax.rem(lax.div(lane, SIDE), 4)
    ranks = []
    for group in range(GROUPS):
        rank = jnp.full((SIDE, DEPTH), order_s[0, group], jnp.int32)
        for view in range(1, VIEWS):
            rank = jnp.where(view_of == view, order_s[view, group], rank)
        ranks.append(rank)
    is_depth = kind_of == 3

    exchange_in = pltpu.make_async_remote_copy(
        src_ref=piece_recv.at[pl.ds(0, GROUPS - 1)],
        dst_ref=piece_recv.at[pl.ds(0, GROUPS - 1)],
        send_sem=piece_send_sem,
        recv_sem=piece_recv_sem,
        device_id=(gx, gy_lo),
        device_id_type=MESH,
    )
    exchange_in.wait_recv()

    depths = []
    for group in range(GROUPS):
        value = jnp.where(is_depth, piece_recv[group], 0.0)
        value = value + pltpu.roll(value, DEPTH - SIDE, 1)
        depths.append(value + pltpu.roll(value, DEPTH - 2 * SIDE, 1))
    fronts = [jnp.zeros((SIDE, DEPTH), F32)] * GROUPS
    for one in range(GROUPS):
        for two in range(one + 1, GROUPS):
            before = ranks[two] < ranks[one]
            fronts[one] = fronts[one] + jnp.where(before, depths[two], 0.0)
            fronts[two] = fronts[two] + jnp.where(before, 0.0, depths[one])
    color = sum(jnp.exp(-fronts[group]) * piece_recv[group] for group in range(GROUPS))
    opaque = 1.0 - jnp.exp(-sum(depths))
    image_v[...] = jnp.transpose(jnp.where(is_depth, opaque, color))
    stores.append(pltpu.make_async_copy(image_v, image_out, out_sem.at[2]))
    stores[2].start()
    for copy in whole:
        copy.wait_send()
    exchange_in.wait_send()
    for copy in stores:
        copy.wait()


def shards(head, temp, category, ice, *params):
    gx_count, gy_count = lax.axis_size("gx"), lax.axis_size("gy")
    rows = SIDE * SIDE
    flat = [a.reshape(rows, DEPTH) for a in (head, temp, category, ice)]
    vmem = pltpu.VMEM
    dma = pltpu.SemaphoreType.DMA
    head, temp, image = pl.pallas_call(
        functools.partial(kernel, gx_count, gy_count),
        out_shape=(
            jax.ShapeDtypeStruct((rows, DEPTH), F32),
            jax.ShapeDtypeStruct((rows, DEPTH), F32),
            jax.ShapeDtypeStruct((DEPTH, SIDE), F32),
        ),
        in_specs=[pl.BlockSpec(memory_space=pl.ANY)] * 10,
        out_specs=[pl.BlockSpec(memory_space=pl.ANY)] * 3,
        scratch_shapes=[
            vmem((rows, DEPTH), F32),
            vmem((rows, DEPTH), F32),
            vmem((rows, DEPTH), jnp.int32),
            vmem((rows, DEPTH), jnp.int32),
            pltpu.SMEM((SOILS,), F32),
            pltpu.SMEM((SOILS,), F32),
            pltpu.SMEM((VIEWS,), F32),
            pltpu.SMEM((3,), F32),
            pltpu.SMEM((3,), F32),
            pltpu.SMEM((VIEWS, GROUPS), jnp.int32),
            vmem((2, 7 * SIDE, DEPTH), F32),
            vmem((2, 7 * SIDE, DEPTH), F32),
            vmem((2, 7 * SIDE, DEPTH), F32),
            vmem((2, 7 * SIDE, DEPTH), F32),
            vmem((4, 4, DEPTH), F32),
            vmem((4, 4, DEPTH), F32),
            vmem((4, 3, SIDE, DEPTH), F32),
            vmem((rows, DEPTH), F32),
            vmem((rows, DEPTH), F32),
            vmem((DEPTH, DEPTH), F32),
            vmem((GROUPS, SIDE, DEPTH), F32),
            vmem((DEPTH, SIDE), F32),
            dma((4,)),
            dma((6,)),
            dma((3,)),
            dma((3,)),
            dma(()),
            dma(()),
            dma((3,)),
        ],
        compiler_params=pltpu.CompilerParams(collective_id=0, has_side_effects=True),
        name="step_and_view",
    )(*flat, *params)
    shape = (SIDE, SIDE, DEPTH)
    return head.reshape(shape), temp.reshape(shape), image.reshape(VIEWS, 4, SIDE, SIDE)


def solution(mesh):
    block = P("gx", "gy", None)
    return jax.shard_map(
        shards,
        mesh=mesh,
        in_specs=(block,) * 4 + (P(),) * 6,
        out_specs=(block, block, P(None, None, "gx", "gy")),
        check_vma=False,
    )
```

time: 105 us -> 36.1 us (0.34); the launches traced: 104 us -> 35.9 us
  other arithmetic: 39.3 us -> 0 us
  Pallas kernels: 0 us -> 32.6 us
  local copies, waits for them, and re-layouts: 30 us -> 2.66 us
  starting transfers between devices: 19.9 us -> 0 us
  blocking collectives: 9.07 us -> 0 us
  waiting for transfers between devices: 3.87 us -> 0 us
    pallas_call x0 -> x1, Pallas kernels: none -> 32.6 us  [shards(): pl.pallas_call(functools.partial(kernel, gx_count, gy_count), out_shape=(...]
    ppermute x4 -> x0, starting transfers between devices: 19.9 us -> none  [the longest x2 13.7 us: with_halo(): after = lax.ppermute(first, axis, down)]
    another operation x5 -> x0, other arithmetic: 15.5 us -> none  [the longest x4 15.5 us: render(): before = jnp.cumsum(optical, axis=2) - optical]
    unnamed x2 -> x0, other arithmetic: 15.2 us -> none
    gather x16 -> x0, local copies, waits for them, and re-layouts: 12.1 us -> none  [the longest x8 6.08 us: plane_slices(): lower_part = lax.dynamic_slice_in_dim(column, start, depth_z, 1)]
    all_to_all x1 -> x0, blocking collectives: 9.07 us -> none  [shards(): lax.all_to_all(pieces[None], 'gy', split_axis=4, concat_axis=0, tiled=True)]
    slice x8 -> x0, local copies, waits for them, and re-layouts: 5.33 us -> none  [the longest x4 2.75 us: render(): gain[color] * (sample - middle[color])]
    ppermute x4 -> x0, waiting for transfers between devices: 3.87 us -> none  [the longest x2 3.86 us: with_halo(): after = lax.ppermute(first, axis, down)]
  transfers between devices with their start and end apart: 4 -> 0, of which waited for: 2 -> 0; matrix products, arithmetic and copies ran while one was open for 1% -> 0% of each run, Pallas kernels for 0% -> 0%
where the time goes in v1:
time: 36.1 us; the launch traced here: 35.9 us
  Pallas kernels  32.6 us (90%)
  local copies, waits for them, and re-layouts  2.66 us (7%)
  between operations  0.66 us (2%)
    pallas_call x1, Pallas kernels, shards(): pl.pallas_call(functools.partial(kernel, gx_count, gy_count), out_shape=(...  32.6 us
    unnamed x7, local copies, waits for them, and re-layouts  2.66 us

profile of v1, /device:TPU:1, one launch (start us, length us, event | category | flops | bytes accessed | tf_op | source)
XLA Modules:
  0.0 35.9 jit_solution(17673470947061508341)
XLA Ops:
  0.6 32.6 %step_and_view.1 = (f32[64,128]{1,0:T(8,128)}, f32[64,128]{1,0:T(8,128)}, f32[128,8]{1,0:T(8,128)}) custom-call(f32[64,128]{1,0:T(8,128)} %bitcast.10, f32[64,128]{1,0:T(8,128)} %bitcast.11, s32[64,128]{1,0:T(8,128)} %bitcast.12, s32[64,128]{1,0:T(8,128)} %bitcast.13, f32[12]{0:T(128)} %ks_in.1, f32[12]{0:T(128)} %alpha_in.1, f32[4]{0:T(128)} %skew_in.1, ...), custom_call_target="tpu_custom_call" | custom-call | tf_op jit(solution)/shard_map/step_and_view/pallas_call | solution.py:433
  33.2 0.0 copy-start.1
  33.2 0.0 copy-start
  33.2 1.4 %copy.16 = f32[8,8,128]{2,1,0:T(8,128)} copy(f32[8,8,128]{2,1,0:T(8,128)} %bitcast.9) | data formatting | bytes 65536
  34.6 0.0 copy-done.1
  34.6 0.6 %copy.17 = f32[8,8,128]{2,1,0:T(8,128)} copy(f32[8,8,128]{2,1,0:T(8,128)S(1)} %bitcast.8) | data formatting | bytes 65536
  35.3 0.0 copy-done
  35.3 0.6 %copy.18 = f32[4,4,8,8]{3,2,1,0:T(8,128)} copy(f32[4,4,8,8]{3,2,1,0:T(8,128)S(1)} %bitcast.7) | data formatting | bytes 8192
Async XLA Ops:
  33.2 1.4 %copy-start.1 = (f32[64,128]{1,0:T(8,128)S(1)}, f32[64,128]{1,0:T(8,128)}, u32[]{:S(2)}) copy-start(f32[64,128]{1,0:T(8,128)} %get-tuple-element.7) | copy-start | bytes 98308
  33.2 2.0 %copy-start = (f32[128,8]{1,0:T(8,128)S(1)}, f32[128,8]{1,0:T(8,128)}, u32[]{:S(2)}) copy-start(f32[128,8]{1,0:T(8,128)} %get-tuple-element.8) | copy-start | bytes 12292

commit v2 on v1

--- a/solution.py
+++ b/solution.py
@@ -52,9 +52,9 @@
     steep_in,
     mid_in,
     order_in,
-    head_out,
-    temp_out,
-    image_out,
+    head_v,
+    temp_v,
+    image_v,
     head_a,
     temp_a,
     cat_a,
@@ -72,18 +72,14 @@
     c_send,
     c_recv,
     ghost,
-    head_v,
-    temp_v,
     piece_send,
     piece_recv,
-    image_v,
     in_sem,
     par_sem,
     halo_send_sem,
     halo_recv_sem,
     piece_send_sem,
     piece_recv_sem,
-    out_sem,
 ):
     gx, gy = lax.axis_index("gx"), lax.axis_index("gy")
     gx_lo, gx_hi = lax.rem(gx + gx_count - 1, gx_count), lax.rem(gx + 1, gx_count)
@@ -117,12 +113,23 @@
         key=lambda d: -(min(d[0], 4 - d[0]) + min(d[1], 4 - d[1])),
     )
     peers = [lax.rem(px + dx, 4) * 4 + lax.rem(py + dy, 4) for dx, dy in shifts]
-    corners = ((gx_lo, gy_lo), (gx_lo, gy_hi), (gx_hi, gy_lo), (gx_hi, gy_hi))
 
     barrier = pltpu.get_barrier_semaphore()
-    greeted = [(gx, peer) for peer in peers] + [*corners, (gx_lo, gy), (gx_hi, gy)]
-    for device in greeted:
+
+    def greet(device):
         pl.semaphore_signal(barrier, inc=1, device_id=device, device_id_type=MESH)
+
+    has_x = (gx > 0, gx < gx_count - 1)
+    has_y = (gy > 0, gy < gy_count - 1)
+    for side, x in enumerate((gx_lo, gx_hi)):
+
+        @pl.when(has_x[side])
+        def _():
+            for y in (gy_lo, gy_hi, gy):
+                greet((x, y))
+
+    for peer in peers:
+        greet((gx, peer))
 
     row = lax.broadcasted_iota(jnp.int32, (SIDE, DEPTH), 0)
     lane = lax.broadcasted_iota(jnp.int32, (SIDE, DEPTH), 1)
@@ -172,44 +179,66 @@
             x_send[side, pl.ds(number * SIDE, SIDE), :] = part
     for number, (x, y) in enumerate(((0, 0), (0, 7), (7, 0), (7, 7))):
         for field, part in enumerate((head[y], temp[y], conduct[y], conduct[y])):
-            c_send[number, pl.ds(field, 1), :] = part[x : x + 1, :]
-
-    pl.semaphore_wait(barrier, len(greeted))
-
-    def remote(src, dst, number, device):
+            c_send[number // 2, number % 2, pl.ds(field, 1), :] = part[x : x + 1, :]
+
+    one_sided = jnp.logical_or(gx == 0, gx == gx_count - 1)
+    pl.semaphore_wait(barrier, len(peers) + jnp.where(one_sided, 3, 6))
+
+    def remote(src, dst, mine, theirs, device):
         return pltpu.make_async_remote_copy(
             src_ref=src,
             dst_ref=dst,
-            send_sem=halo_send_sem.at[number],
-            recv_sem=halo_recv_sem.at[number],
+            send_sem=halo_send_sem.at[mine],
+            recv_sem=halo_recv_sem.at[theirs],
             device_id=device,
             device_id_type=MESH,
         )
 
-    for number, device in enumerate(corners):
-        remote(c_send.at[number], c_recv.at[3 - number], 0, device).start()
-    remote(y_send.at[0], y_recv.at[1], 1, (gx, gy_lo)).start()
-    remote(y_send.at[1], y_recv.at[0], 1, (gx, gy_hi)).start()
-    remote(x_send.at[0], x_recv.at[1], 2, (gx_lo, gy)).start()
-    remote(x_send.at[1], x_recv.at[0], 2, (gx_hi, gy)).start()
+    x_copies = []
+    for side, x in enumerate((gx_lo, gx_hi)):
+        copies = [
+            remote(c_send.at[side, ys], c_recv.at[1 - side, 1 - ys], 3 + side, 4 - side, (x, y))
+            for ys, y in enumerate((gy_lo, gy_hi))
+        ]
+        copies.append(remote(x_send.at[side], x_recv.at[1 - side], 1 + side, 2 - side, (x, gy)))
+        x_copies.append(copies)
+
+        @pl.when(has_x[side])
+        def _():
+            for copy in copies[:2]:
+                copy.start()
+
+    remote(y_send.at[0], y_recv.at[1], 0, 0, (gx, gy_lo)).start()
+    remote(y_send.at[1], y_recv.at[0], 0, 0, (gx, gy_hi)).start()
+    for side in range(2):
+
+        @pl.when(has_x[side])
+        def _():
+            x_copies[side][2].start()
 
     for copy in params[2:]:
         copy.wait()
 
-    has_x = (gx > 0, gx < gx_count - 1)
-    has_y = (gy > 0, gy < gy_count - 1)
     x_open = (jnp.logical_or(row > 0, has_x[0]), jnp.logical_or(row < SIDE - 1, has_x[1]))
     y_open = (jnp.logical_or(row > 0, has_y[0]), jnp.logical_or(row < SIDE - 1, has_y[1]))
 
     own_vertical = [vertical(head[y], temp[y], conduct[y], lane) for y in range(SIDE)]
 
-    whole = (
-        remote(c_send, c_recv, 0, (gx, gy_lo)),
-        remote(y_send, y_recv, 1, (gx, gy_lo)),
-        remote(x_send, x_recv, 2, (gx, gy_lo)),
-    )
-    for copy in whole:
-        copy.wait_recv()
+    whole_y = remote(y_send, y_recv, 0, 0, (gx, gy_lo))
+    whole_x = [
+        (
+            remote(x_send.at[side], x_recv.at[side], 1 + side, 1 + side, (gx, gy_lo)),
+            remote(c_send.at[side], c_recv.at[side], 3 + side, 3 + side, (gx, gy_lo)),
+        )
+        for side in range(2)
+    ]
+    whole_y.wait_recv()
+    for side in range(2):
+
+        @pl.when(has_x[side])
+        def _():
+            for copy in whole_x[side]:
+                copy.wait_recv()
 
     def along_rows(value, before, after):
         return (
@@ -238,11 +267,10 @@
         return jnp.where(present, value, 0.0)
 
     def corner(xs, ys):
-        number = 2 * xs + ys
         return (
-            c_recv[number, pl.ds(0, 1), :],
-            warm_if(jnp.logical_and(has_x[xs], has_y[ys]), c_recv[number, pl.ds(1, 1), :]),
-            c_recv[number, pl.ds(2, 1), :],
+            c_recv[xs, ys, pl.ds(0, 1), :],
+            warm_if(jnp.logical_and(has_x[xs], has_y[ys]), c_recv[xs, ys, pl.ds(1, 1), :]),
+            c_recv[xs, ys, pl.ds(2, 1), :],
         )
 
     y_ghost, x_ghost = [], []
@@ -327,12 +355,6 @@
     for y in range(SIDE):
         head_v[pl.ds(y, SIDE, stride=SIDE), :] = head[y]
         temp_v[pl.ds(y, SIDE, stride=SIDE), :] = temp[y]
-    stores = [
-        pltpu.make_async_copy(head_v, head_out, out_sem.at[0]),
-        pltpu.make_async_copy(temp_v, temp_out, out_sem.at[1]),
-    ]
-    for copy in stores:
-        copy.start()
 
     theta = [0.05 + 0.4 * jnp.exp(0.8 * jnp.minimum(h, 0.0)) for h in head]
     planes_all = gy_count * SIDE
@@ -415,12 +437,27 @@
     color = sum(jnp.exp(-fronts[group]) * piece_recv[group] for group in range(GROUPS))
     opaque = 1.0 - jnp.exp(-sum(depths))
     image_v[...] = jnp.transpose(jnp.where(is_depth, opaque, color))
-    stores.append(pltpu.make_async_copy(image_v, image_out, out_sem.at[2]))
-    stores[2].start()
-    for copy in whole:
-        copy.wait_send()
+    whole_y.wait_send()
+    for side in range(2):
+
+        @pl.when(has_x[side])
+        def _():
+            for copy in whole_x[side]:
+                copy.wait_send()
+
     exchange_in.wait_send()
-    for copy in stores:
+
+
+def put_out(head_v, temp_v, image_v, head_out, temp_out, image_out, sem):
+    copies = [
+        pltpu.make_async_copy(src, dst, sem.at[number])
+        for number, (src, dst) in enumerate(
+            ((image_v, image_out), (head_v, head_out), (temp_v, temp_out))
+        )
+    ]
+    for copy in copies:
+        copy.start()
+    for copy in copies:
         copy.wait()
 
 
@@ -430,15 +467,12 @@
     flat = [a.reshape(rows, DEPTH) for a in (head, temp, category, ice)]
     vmem = pltpu.VMEM
     dma = pltpu.SemaphoreType.DMA
-    head, temp, image = pl.pallas_call(
+    shapes = ((rows, DEPTH), (rows, DEPTH), (DEPTH, SIDE))
+    results = pl.pallas_call(
         functools.partial(kernel, gx_count, gy_count),
-        out_shape=(
-            jax.ShapeDtypeStruct((rows, DEPTH), F32),
-            jax.ShapeDtypeStruct((rows, DEPTH), F32),
-            jax.ShapeDtypeStruct((DEPTH, SIDE), F32),
-        ),
+        out_shape=tuple(pltpu.VMEM(shape, F32) for shape in shapes),
         in_specs=[pl.BlockSpec(memory_space=pl.ANY)] * 10,
-        out_specs=[pl.BlockSpec(memory_space=pl.ANY)] * 3,
+        out_specs=[pl.BlockSpec(memory_space=pltpu.VMEM)] * 3,
         scratch_shapes=[
             vmem((rows, DEPTH), F32),
             vmem((rows, DEPTH), F32),
@@ -454,25 +488,29 @@
             vmem((2, 7 * SIDE, DEPTH), F32),
             vmem((2, 7 * SIDE, DEPTH), F32),
             vmem((2, 7 * SIDE, DEPTH), F32),
-            vmem((4, 4, DEPTH), F32),
-            vmem((4, 4, DEPTH), F32),
+            vmem((2, 2, 4, DEPTH), F32),
+            vmem((2, 2, 4, DEPTH), F32),
             vmem((4, 3, SIDE, DEPTH), F32),
-            vmem((rows, DEPTH), F32),
-            vmem((rows, DEPTH), F32),
             vmem((DEPTH, DEPTH), F32),
             vmem((GROUPS, SIDE, DEPTH), F32),
-            vmem((DEPTH, SIDE), F32),
             dma((4,)),
             dma((6,)),
-            dma((3,)),
-            dma((3,)),
+            dma((5,)),
+            dma((5,)),
             dma(()),
             dma(()),
-            dma((3,)),
         ],
         compiler_params=pltpu.CompilerParams(collective_id=0, has_side_effects=True),
         name="step_and_view",
     )(*flat, *params)
+    head, temp, image = pl.pallas_call(
+        put_out,
+        out_shape=tuple(jax.ShapeDtypeStruct(shape, F32) for shape in shapes),
+        in_specs=[pl.BlockSpec(memory_space=pltpu.VMEM)] * 3,
+        out_specs=[pl.BlockSpec(memory_space=pl.ANY)] * 3,
+        scratch_shapes=[dma((3,))],
+        name="put_out",
+    )(*(pltpu.with_memory_space_constraint(r, pltpu.VMEM) for r in results))
     shape = (SIDE, SIDE, DEPTH)
     return head.reshape(shape), temp.reshape(shape), image.reshape(VIEWS, 4, SIDE, SIDE)
 

time: 36.1 us -> 26.3 us (0.73)
  Pallas kernels: 32.6 us -> 25.4 us
  local copies, waits for them, and re-layouts: 2.66 us -> 0 us
    pallas_call x1 -> x2, Pallas kernels: 32.6 us -> 25.4 us  [the longest x1 24.8 us: shards(): pl.pallas_call(functools.partial(kernel, gx_count, gy_count), out_shape=t...]
    unnamed x7 -> x0, local copies, waits for them, and re-layouts: 2.66 us -> none
where the time goes in v2:
time: 26.3 us; the launch traced here: 26.1 us
  Pallas kernels  25.4 us (97%)
  between operations  0.64 us (2%)
    pallas_call x1, Pallas kernels, shards(): pl.pallas_call(functools.partial(kernel, gx_count, gy_count), out_shape=t...  24.8 us
    pallas_call x1, Pallas kernels, shards(): pl.pallas_call(put_out, out_shape=tuple((jax.ShapeDtypeStruct(shape, F32)...  0.67 us

profile of v2, /device:TPU:1, one launch (start us, length us, event | category | flops | bytes accessed | tf_op | source)
XLA Modules:
  0.0 26.1 jit_solution(17993636085886436418)
XLA Ops:
  0.6 24.8 %step_and_view.1 = (f32[64,128]{1,0:T(8,128)S(1)}, f32[64,128]{1,0:T(8,128)S(1)}, f32[128,8]{1,0:T(8,128)S(1)}) custom-call(f32[64,128]{1,0:T(8,128)} %bitcast.7, f32[64,128]{1,0:T(8,128)} %bitcast.8, s32[64,128]{1,0:T(8,128)} %bitcast.9, s32[64,128]{1,0:T(8,128)} %bitcast.10, f32[12]{0:T(128)} %ks_in.1, f32[12]{0:T(128)} %alpha_in.1, f32[4]{0:T(128)} %skew_in.1, ...), custom_call_target="tpu_custom_call" | custom-call | tf_op jit(solution)/shard_map/step_and_view/pallas_call | solution.py:471
  25.4 0.7 %put_out.1 = (f32[64,128]{1,0:T(8,128)}, f32[64,128]{1,0:T(8,128)}, f32[128,8]{1,0:T(8,128)}) custom-call(f32[64,128]{1,0:T(8,128)S(1)} %get-tuple-element.9.head_v, f32[64,128]{1,0:T(8,128)S(1)} %get-tuple-element.10.temp_v, f32[128,8]{1,0:T(8,128)S(1)} %get-tuple-element.11.image_v), custom_call_target="tpu_custom_call" | custom-call | tf_op jit(solution)/shard_map/put_out/pallas_call | solution.py:506

commit v3 on v2

--- a/solution.py
+++ b/solution.py
@@ -78,6 +78,7 @@
     par_sem,
     halo_send_sem,
     halo_recv_sem,
+    known_sem,
     piece_send_sem,
     piece_recv_sem,
 ):
@@ -114,22 +115,41 @@
     )
     peers = [lax.rem(px + dx, 4) * 4 + lax.rem(py + dy, 4) for dx, dy in shifts]
 
+    has_x = (gx > 0, gx < gx_count - 1)
+    has_y = (gy > 0, gy < gy_count - 1)
+    x_at, y_at = (gx_lo, gx_hi), (gy_lo, gy_hi)
+    both = [[jnp.logical_and(has_x[a], has_y[b]) for b in range(2)] for a in range(2)]
+    hub = 1 + lax.rem(gx, 2)
+    is_hub = gy == hub
+    far_from_hub = jnp.abs(gy - hub) > 1
+
     barrier = pltpu.get_barrier_semaphore()
 
     def greet(device):
         pl.semaphore_signal(barrier, inc=1, device_id=device, device_id_type=MESH)
 
-    has_x = (gx > 0, gx < gx_count - 1)
-    has_y = (gy > 0, gy < gy_count - 1)
-    for side, x in enumerate((gx_lo, gx_hi)):
-
-        @pl.when(has_x[side])
+    for a in range(2):
+        for b in range(2):
+
+            @pl.when(both[a][b])
+            def _():
+                greet((x_at[a], y_at[b]))
+
+    for b in range(2):
+
+        @pl.when(has_y[b])
         def _():
-            for y in (gy_lo, gy_hi, gy):
-                greet((x, y))
-
-    for peer in peers:
-        greet((gx, peer))
+            greet((gx, y_at[b]))
+
+    @pl.when(far_from_hub)
+    def _():
+        greet((gx, hub))
+
+    for a in range(2):
+
+        @pl.when(has_x[a])
+        def _():
+            greet((x_at[a], gy))
 
     row = lax.broadcasted_iota(jnp.int32, (SIDE, DEPTH), 0)
     lane = lax.broadcasted_iota(jnp.int32, (SIDE, DEPTH), 1)
@@ -181,8 +201,12 @@
         for field, part in enumerate((head[y], temp[y], conduct[y], conduct[y])):
             c_send[number // 2, number % 2, pl.ds(field, 1), :] = part[x : x + 1, :]
 
-    one_sided = jnp.logical_or(gx == 0, gx == gx_count - 1)
-    pl.semaphore_wait(barrier, len(peers) + jnp.where(one_sided, 3, 6))
+    def count(flags):
+        return sum(flag.astype(jnp.int32) for flag in flags)
+
+    x_sides, y_sides = count(has_x), count(has_y)
+    gathered = jnp.where(is_hub, gy_count - 3, 0)
+    pl.semaphore_wait(barrier, gathered + y_sides + x_sides * (1 + y_sides))
 
     def remote(src, dst, mine, theirs, device):
         return pltpu.make_async_remote_copy(
@@ -194,27 +218,31 @@
             device_id_type=MESH,
         )
 
-    x_copies = []
-    for side, x in enumerate((gx_lo, gx_hi)):
-        copies = [
-            remote(c_send.at[side, ys], c_recv.at[1 - side, 1 - ys], 3 + side, 4 - side, (x, y))
-            for ys, y in enumerate((gy_lo, gy_hi))
-        ]
-        copies.append(remote(x_send.at[side], x_recv.at[1 - side], 1 + side, 2 - side, (x, gy)))
-        x_copies.append(copies)
-
-        @pl.when(has_x[side])
+    def y_copy(b):
+        return remote(y_send.at[b], y_recv.at[1 - b], b, 1 - b, (gx, y_at[b]))
+
+    def x_copy(a):
+        return remote(x_send.at[a], x_recv.at[1 - a], 2 + a, 3 - a, (x_at[a], gy))
+
+    def c_copy(a, b):
+        slot = 4 + 2 * a + b
+        return remote(
+            c_send.at[a, b], c_recv.at[1 - a, 1 - b], slot, 11 - slot, (x_at[a], y_at[b])
+        )
+
+    copies = [(both[a][b], c_copy(a, b)) for a in range(2) for b in range(2)]
+    copies += [(has_y[b], y_copy(b)) for b in range(2)]
+    copies += [(has_x[a], x_copy(a)) for a in range(2)]
+    for present, copy in copies:
+
+        @pl.when(present)
         def _():
-            for copy in copies[:2]:
-                copy.start()
-
-    remote(y_send.at[0], y_recv.at[1], 0, 0, (gx, gy_lo)).start()
-    remote(y_send.at[1], y_recv.at[0], 0, 0, (gx, gy_hi)).start()
-    for side in range(2):
-
-        @pl.when(has_x[side])
-        def _():
-            x_copies[side][2].start()
+            copy.start()
+
+    @pl.when(is_hub)
+    def _():
+        for peer in peers:
+            pl.semaphore_signal(known_sem, inc=1, device_id=(gx, peer), device_id_type=MESH)
 
     for copy in params[2:]:
         copy.wait()
@@ -224,21 +252,18 @@
 
     own_vertical = [vertical(head[y], temp[y], conduct[y], lane) for y in range(SIDE)]
 
-    whole_y = remote(y_send, y_recv, 0, 0, (gx, gy_lo))
-    whole_x = [
-        (
-            remote(x_send.at[side], x_recv.at[side], 1 + side, 1 + side, (gx, gy_lo)),
-            remote(c_send.at[side], c_recv.at[side], 3 + side, 3 + side, (gx, gy_lo)),
-        )
-        for side in range(2)
-    ]
-    whole_y.wait_recv()
-    for side in range(2):
-
-        @pl.when(has_x[side])
+    def arrived(a, b):
+        slot = 4 + 2 * a + b
+        return remote(c_send.at[a, b], c_recv.at[a, b], slot, slot, (gx, gy_lo))
+
+    waits = [(has_x[a], remote(x_send.at[a], x_recv.at[a], 2 + a, 2 + a, (gx, gy_lo))) for a in range(2)]
+    waits += [(both[a][b], arrived(a, b)) for a in range(2) for b in range(2)]
+    waits += [(has_y[b], remote(y_send.at[b], y_recv.at[b], b, b, (gx, gy_lo))) for b in range(2)]
+    for present, copy in waits:
+
+        @pl.when(present)
         def _():
-            for copy in whole_x[side]:
-                copy.wait_recv()
+            copy.wait_recv()
 
     def along_rows(value, before, after):
         return (
@@ -395,6 +420,10 @@
             device_id_type=MESH,
         )
 
+    @pl.when(jnp.logical_not(is_hub))
+    def _():
+        pl.semaphore_wait(known_sem, 1)
+
     for peer in peers:
         exchange(
             piece_send.at[pl.ds(pl.multiple_of(peer * SIDE, SIDE), SIDE)],
@@ -437,13 +466,11 @@
     color = sum(jnp.exp(-fronts[group]) * piece_recv[group] for group in range(GROUPS))
     opaque = 1.0 - jnp.exp(-sum(depths))
     image_v[...] = jnp.transpose(jnp.where(is_depth, opaque, color))
-    whole_y.wait_send()
-    for side in range(2):
-
-        @pl.when(has_x[side])
+    for present, copy in waits:
+
+        @pl.when(present)
         def _():
-            for copy in whole_x[side]:
-                copy.wait_send()
+            copy.wait_send()
 
     exchange_in.wait_send()
 
@@ -495,8 +522,9 @@
             vmem((GROUPS, SIDE, DEPTH), F32),
             dma((4,)),
             dma((6,)),
-            dma((5,)),
-            dma((5,)),
+            dma((8,)),
+            dma((8,)),
+            pltpu.SemaphoreType.REGULAR(()),
             dma(()),
             dma(()),
         ],

time: 26.3 us -> 23.7 us (0.901)
  Pallas kernels: 25.4 us -> 22.8 us
    pallas_call x1, Pallas kernels: 24.8 us -> 22.1 us  [shards(): pl.pallas_call(functools.partial(kernel, gx_count, gy_count), out_shape=t...]
where the time goes in v3:
time: 23.7 us; the launch traced here: 23.4 us
  Pallas kernels  22.8 us (96%)
  between operations  0.64 us (3%)
    pallas_call x1, Pallas kernels, shards(): pl.pallas_call(functools.partial(kernel, gx_count, gy_count), out_shape=t...  22.1 us
    pallas_call x1, Pallas kernels, shards(): pl.pallas_call(put_out, out_shape=tuple((jax.ShapeDtypeStruct(shape, F32)...  0.67 us

profile of v3, /device:TPU:1, one launch (start us, length us, event | category | flops | bytes accessed | tf_op | source)
XLA Modules:
  0.0 23.4 jit_solution(3818174647095651011)
XLA Ops:
  0.6 22.1 %step_and_view.1 = (f32[64,128]{1,0:T(8,128)S(1)}, f32[64,128]{1,0:T(8,128)S(1)}, f32[128,8]{1,0:T(8,128)S(1)}) custom-call(f32[64,128]{1,0:T(8,128)} %bitcast.7, f32[64,128]{1,0:T(8,128)} %bitcast.8, s32[64,128]{1,0:T(8,128)} %bitcast.9, s32[64,128]{1,0:T(8,128)} %bitcast.10, f32[12]{0:T(128)} %ks_in.1, f32[12]{0:T(128)} %alpha_in.1, f32[4]{0:T(128)} %skew_in.1, ...), custom_call_target="tpu_custom_call" | custom-call | tf_op jit(solution)/shard_map/step_and_view/pallas_call | solution.py:498
  22.8 0.7 %put_out.1 = (f32[64,128]{1,0:T(8,128)}, f32[64,128]{1,0:T(8,128)}, f32[128,8]{1,0:T(8,128)}) custom-call(f32[64,128]{1,0:T(8,128)S(1)} %get-tuple-element.9.head_v, f32[64,128]{1,0:T(8,128)S(1)} %get-tuple-element.10.temp_v, f32[128,8]{1,0:T(8,128)S(1)} %get-tuple-element.11.image_v), custom_call_target="tpu_custom_call" | custom-call | tf_op jit(solution)/shard_map/put_out/pallas_call | solution.py:534

commit v4 on v3

--- a/solution.py
+++ b/solution.py
@@ -14,6 +14,8 @@
 DEPTH = 128
 GROUPS = 16
 DIFFUSE = 0.12
+HUB = 1
+BEFORE, CROSS, BELOW, DIAGONAL, MOST, ALL = range(6)
 F32 = jnp.float32
 
 
@@ -74,12 +76,9 @@
     ghost,
     piece_send,
     piece_recv,
-    in_sem,
-    par_sem,
-    halo_send_sem,
+    local_sem,
     halo_recv_sem,
     known_sem,
-    piece_send_sem,
     piece_recv_sem,
 ):
     gx, gy = lax.axis_index("gx"), lax.axis_index("gy")
@@ -87,13 +86,13 @@
     gy_lo, gy_hi = lax.rem(gy + gy_count - 1, gy_count), lax.rem(gy + 1, gy_count)
 
     loads = [
-        pltpu.make_async_copy(src, dst, in_sem.at[number])
+        pltpu.make_async_copy(src, dst, local_sem.at[number])
         for number, (src, dst) in enumerate(
             ((head_in, head_a), (temp_in, temp_a), (cat_in, cat_a), (ice_in, ice_a))
         )
     ]
     params = [
-        pltpu.make_async_copy(src, dst, par_sem.at[number])
+        pltpu.make_async_copy(src, dst, local_sem.at[4 + number])
         for number, (src, dst) in enumerate(
             (
                 (ks_in, ks_s),
@@ -119,45 +118,74 @@
     has_y = (gy > 0, gy < gy_count - 1)
     x_at, y_at = (gx_lo, gx_hi), (gy_lo, gy_hi)
     both = [[jnp.logical_and(has_x[a], has_y[b]) for b in range(2)] for a in range(2)]
-    hub = 1 + lax.rem(gx, 2)
-    is_hub = gy == hub
-    far_from_hub = jnp.abs(gy - hub) > 1
+    is_hub = gy == HUB
+    is_late = gy == HUB - 1
+    far_from_hub = jnp.abs(gy - HUB) > 1
 
     barrier = pltpu.get_barrier_semaphore()
 
     def greet(device):
         pl.semaphore_signal(barrier, inc=1, device_id=device, device_id_type=MESH)
 
+    def tell(number, device):
+        pl.semaphore_signal(known_sem.at[number], inc=1, device_id=device, device_id_type=MESH)
+
     for a in range(2):
-        for b in range(2):
-
-            @pl.when(both[a][b])
+
+        @pl.when(both[a][0])
+        def _():
+            greet((x_at[a], gy_lo))
+
+    @pl.when(has_y[0])
+    def _():
+        greet((gx, gy_lo))
+
+    @pl.when(has_x[0])
+    def _():
+        greet((gx_lo, gy))
+
+    @pl.when(far_from_hub)
+    def _():
+        greet((gx, HUB))
+
+    def one(flag):
+        return flag.astype(jnp.int32)
+
+    x_sides = one(has_x[0]) + one(has_x[1])
+    gathered = jnp.where(is_hub, gy_count - 3, 0)
+    awaited = gathered + one(has_x[1]) + one(has_y[1]) * (1 + x_sides)
+
+    @pl.when(awaited > 0)
+    def _():
+        pl.semaphore_wait(barrier, awaited)
+
+    for a in range(2):
+
+        @pl.when(both[a][1])
+        def _():
+            tell((CROSS, DIAGONAL)[a], (x_at[a], gy_hi))
+
+    @pl.when(has_y[1])
+    def _():
+        tell(BELOW, (gx, gy_hi))
+
+    @pl.when(has_x[1])
+    def _():
+        tell(BEFORE, (gx_hi, gy))
+
+    @pl.when(is_hub)
+    def _():
+        for peer in peers:
+
+            @pl.when(peer != HUB - 1)
             def _():
-                greet((x_at[a], y_at[b]))
-
-    for b in range(2):
-
-        @pl.when(has_y[b])
-        def _():
-            greet((gx, y_at[b]))
-
-    @pl.when(far_from_hub)
-    def _():
-        greet((gx, hub))
-
-    for a in range(2):
-
-        @pl.when(has_x[a])
-        def _():
-            greet((x_at[a], gy))
+                tell(MOST, (gx, peer))
 
     row = lax.broadcasted_iota(jnp.int32, (SIDE, DEPTH), 0)
     lane = lax.broadcasted_iota(jnp.int32, (SIDE, DEPTH), 1)
     first, last = row == 0, row == SIDE - 1
 
-    for copy in params[:2]:
-        copy.wait()
-    for copy in loads:
+    for copy in params + loads:
         copy.wait()
 
     def across(ref, y):
@@ -166,15 +194,16 @@
     def tile(ref, x):
         return ref[pl.ds(x * SIDE, SIDE), :]
 
-    head = [across(head_a, y) for y in range(SIDE)]
-    temp = [across(temp_a, y) for y in range(SIDE)]
-    category = [across(cat_a, y) for y in range(SIDE)]
-    ice = [across(ice_a, y).astype(F32) for y in range(SIDE)]
-    ks = [lookup(category[y], ks_s) for y in range(SIDE)]
-    alpha = [lookup(category[y], alpha_s) for y in range(SIDE)]
-    conduct = [
-        conductivity(head[y], temp[y], ks[y], alpha[y], ice[y]) for y in range(SIDE)
-    ]
+    head, temp, category, ice, ks, alpha, conduct = ({} for _ in range(7))
+
+    def own(y):
+        head[y], temp[y], category[y] = across(head_a, y), across(temp_a, y), across(cat_a, y)
+        ice[y] = across(ice_a, y).astype(F32)
+        ks[y], alpha[y] = lookup(category[y], ks_s), lookup(category[y], alpha_s)
+        conduct[y] = conductivity(head[y], temp[y], ks[y], alpha[y], ice[y])
+
+    for y in (0, 1, SIDE - 2, SIDE - 1):
+        own(y)
     edge = {}
     for x in (0, 1, SIDE - 2, SIDE - 1):
         h, t, c = tile(head_a, x), tile(temp_a, x), tile(cat_a, x)
@@ -201,18 +230,11 @@
         for field, part in enumerate((head[y], temp[y], conduct[y], conduct[y])):
             c_send[number // 2, number % 2, pl.ds(field, 1), :] = part[x : x + 1, :]
 
-    def count(flags):
-        return sum(flag.astype(jnp.int32) for flag in flags)
-
-    x_sides, y_sides = count(has_x), count(has_y)
-    gathered = jnp.where(is_hub, gy_count - 3, 0)
-    pl.semaphore_wait(barrier, gathered + y_sides + x_sides * (1 + y_sides))
-
     def remote(src, dst, mine, theirs, device):
         return pltpu.make_async_remote_copy(
             src_ref=src,
             dst_ref=dst,
-            send_sem=halo_send_sem.at[mine],
+            send_sem=local_sem.at[mine],
             recv_sem=halo_recv_sem.at[theirs],
             device_id=device,
             device_id_type=MESH,
@@ -230,40 +252,53 @@
             c_send.at[a, b], c_recv.at[1 - a, 1 - b], slot, 11 - slot, (x_at[a], y_at[b])
         )
 
-    copies = [(both[a][b], c_copy(a, b)) for a in range(2) for b in range(2)]
-    copies += [(has_y[b], y_copy(b)) for b in range(2)]
-    copies += [(has_x[a], x_copy(a)) for a in range(2)]
-    for present, copy in copies:
-
+    def send(present, copy, *known):
         @pl.when(present)
         def _():
+            for number in known:
+                pl.semaphore_wait(known_sem.at[number], 1)
             copy.start()
 
+    for a in range(2):
+        send(both[a][1], c_copy(a, 1))
+    send(has_y[1], y_copy(1))
+    send(has_x[1], x_copy(1))
+    send(has_x[0], x_copy(0), BEFORE)
+    send(both[1][0], c_copy(1, 0), CROSS)
+    send(has_y[0], y_copy(0), BELOW)
+
     @pl.when(is_hub)
     def _():
         for peer in peers:
-            pl.semaphore_signal(known_sem, inc=1, device_id=(gx, peer), device_id_type=MESH)
-
-    for copy in params[2:]:
-        copy.wait()
+            tell(ALL, (gx, peer))
+
+    send(both[0][0], c_copy(0, 0), DIAGONAL)
 
     x_open = (jnp.logical_or(row > 0, has_x[0]), jnp.logical_or(row < SIDE - 1, has_x[1]))
     y_open = (jnp.logical_or(row > 0, has_y[0]), jnp.logical_or(row < SIDE - 1, has_y[1]))
 
-    own_vertical = [vertical(head[y], temp[y], conduct[y], lane) for y in range(SIDE)]
+    for y in range(2, SIDE - 2):
+        own(y)
 
     def arrived(a, b):
         slot = 4 + 2 * a + b
         return remote(c_send.at[a, b], c_recv.at[a, b], slot, slot, (gx, gy_lo))
 
-    waits = [(has_x[a], remote(x_send.at[a], x_recv.at[a], 2 + a, 2 + a, (gx, gy_lo))) for a in range(2)]
-    waits += [(both[a][b], arrived(a, b)) for a in range(2) for b in range(2)]
-    waits += [(has_y[b], remote(y_send.at[b], y_recv.at[b], b, b, (gx, gy_lo))) for b in range(2)]
-    for present, copy in waits:
-
-        @pl.when(present)
-        def _():
-            copy.wait_recv()
+    x_waits = [
+        (has_x[a], remote(x_send.at[a], x_recv.at[a], 2 + a, 2 + a, (gx, gy_lo)))
+        for a in range(2)
+    ]
+    y_waits = [(both[a][b], arrived(a, b)) for a in range(2) for b in range(2)]
+    y_waits += [
+        (has_y[b], remote(y_send.at[b], y_recv.at[b], b, b, (gx, gy_lo))) for b in range(2)
+    ]
+
+    def receive(waits):
+        for present, copy in waits:
+
+            @pl.when(present)
+            def _():
+                copy.wait_recv()
 
     def along_rows(value, before, after):
         return (
@@ -298,18 +333,11 @@
             c_recv[xs, ys, pl.ds(2, 1), :],
         )
 
-    y_ghost, x_ghost = [], []
-    for part_of, present, dest in ((y_part, has_y, y_ghost), (x_part, has_x, x_ghost)):
-        for side in range(2):
-            h, t, c, i = (part_of(side, number) for number in range(4))
-            k_s, a = lookup(c, ks_s), lookup(c, alpha_s)
-            k = conductivity(h, t, k_s, a, i)
-            far = tuple(part_of(side, number) for number in range(4, 7))
-            dest.append((h, warm_if(present[side], t), k, k_s, a, i, far))
-
-    for side in range(2):
-        for field in range(3):
-            ghost[side, field] = x_ghost[side][field]
+    def read_ghost(part_of, side, present):
+        h, t, c, i = (part_of(side, number) for number in range(4))
+        k_s, a = lookup(c, ks_s), lookup(c, alpha_s)
+        far = tuple(part_of(side, number) for number in range(4, 7))
+        return h, warm_if(present, t), conductivity(h, t, k_s, a, i), k_s, a, i, far
 
     def step(h, t, change, warm):
         return h + 0.5 * change, t + DIFFUSE * (warm - 6.0 * t)
@@ -317,78 +345,52 @@
     def face(k_a, h_a, k_b, h_b):
         return (k_a + k_b) * (h_b - h_a)
 
-    def ghost_step(cell, inner, ends, opened, present):
-        h, t, k, k_s, a, i, far = cell
+    def ghost_base(cell, inner):
+        h, t, k, far = cell[0], cell[1], cell[2], cell[6]
         change, warm = vertical(h, t, k, lane)
+        change = change + face(k, h, far[2], far[0]) + face(k, h, inner[2], inner[0])
+        return change, warm + far[1] + inner[1]
+
+    def ghost_step(cell, base, ends, opened, present):
+        h, t, k, k_s, a, i, _ = cell
         rows, rows_warm = change_rows(h, k, t, ends, opened)
-        change = change + rows + face(k, h, far[2], far[0]) + face(k, h, inner[2], inner[0])
-        warm = warm + rows_warm + far[1] + inner[1]
-        h, t = step(h, t, change, warm)
+        h, t = step(h, t, base[0] + rows, base[1] + rows_warm)
         return h, warm_if(present, t), conductivity(h, t, k_s, a, i)
 
-    y_next = [
-        ghost_step(
-            y_ghost[side],
-            (head[y], temp[y], conduct[y]),
-            (corner(0, side), corner(1, side)),
-            x_open,
-            has_y[side],
-        )
-        for side, y in ((0, 0), (1, SIDE - 1))
-    ]
-    x_next = [
-        ghost_step(
-            x_ghost[side],
-            (edge[x][0], edge[x][1], edge[x][4]),
-            (corner(side, 0), corner(side, 1)),
-            y_open,
-            has_x[side],
-        )
-        for side, x in ((0, 0), (1, SIDE - 1))
-    ]
-    for side in range(2):
-        for field in range(3):
-            ghost[2 + side, field] = x_next[side][field]
-
-    def main_step(head_, temp_, conduct_, lows, highs, slot, verticals):
-        hs = [lows[0], *head_, highs[0]]
-        ts = [lows[1], *temp_, highs[1]]
-        ks_ = [lows[2], *conduct_, highs[2]]
-        faces = [face(ks_[y], hs[y], ks_[y + 1], hs[y + 1]) for y in range(SIDE + 1)]
-        faces[0] = jnp.where(has_y[0], faces[0], 0.0)
-        faces[SIDE] = jnp.where(has_y[1], faces[SIDE], 0.0)
-        result = []
-        for y in range(SIDE):
-            ends = tuple(
-                tuple(ghost[slot + side, field, pl.ds(y, 1), :] for field in range(3))
-                for side in range(2)
-            )
-            rows, rows_warm = change_rows(head_[y], conduct_[y], temp_[y], ends, x_open)
-            change, warm = verticals[y]
-            change = change + rows + faces[y + 1] - faces[y]
-            warm = warm + rows_warm + ts[y] + ts[y + 2]
-            result.append(step(head_[y], temp_[y], change, warm))
-        return [r[0] for r in result], [r[1] for r in result]
-
-    head, temp = main_step(head, temp, conduct, y_ghost[0], y_ghost[1], 0, own_vertical)
-    conduct = [
-        conductivity(head[y], temp[y], ks[y], alpha[y], ice[y]) for y in range(SIDE)
-    ]
-    verticals = [vertical(head[y], temp[y], conduct[y], lane) for y in range(SIDE)]
-    head, temp = main_step(head, temp, conduct, y_next[0], y_next[1], 2, verticals)
-
-    for y in range(SIDE):
-        head_v[pl.ds(y, SIDE, stride=SIDE), :] = head[y]
-        temp_v[pl.ds(y, SIDE, stride=SIDE), :] = temp[y]
-
-    theta = [0.05 + 0.4 * jnp.exp(0.8 * jnp.minimum(h, 0.0)) for h in head]
+    def keep(slot, cells):
+        for side in range(2):
+            for field in range(3):
+                ghost[slot + side, field] = cells[side][field]
+
+    def base_of(y, h, t, k, slot):
+        ends = tuple(
+            tuple(ghost[slot + side, field, pl.ds(y, 1), :] for field in range(3))
+            for side in range(2)
+        )
+        change, warm = vertical(h[y], t[y], k[y], lane)
+        rows, rows_warm = change_rows(h[y], k[y], t[y], ends, x_open)
+        return change + rows, warm + rows_warm
+
+    def plane_step(y, h, t, k, base, faces):
+        for edge_ in (y, y + 1):
+            if edge_ not in faces:
+                value = face(k[edge_ - 1], h[edge_ - 1], k[edge_], h[edge_])
+                if edge_ in (0, SIDE):
+                    value = jnp.where(has_y[edge_ // SIDE], value, 0.0)
+                faces[edge_] = value
+        return step(
+            h[y],
+            t[y],
+            base[0] + faces[y + 1] - faces[y],
+            base[1] + t[y - 1] + t[y + 1],
+        )
+
     planes_all = gy_count * SIDE
-    layers = []
-    for view in range(VIEWS):
-        clear = None
+
+    def view_planes(view, planes, theta):
+        clear = depth = None
         sums = [None] * 3
-        depth = None
-        for y in range(SIDE):
+        for y in planes:
             shift = skew_s[view] * ((gy * SIDE + y).astype(F32) - 0.5 * planes_all)
             wrapped = shift - DEPTH * jnp.floor(shift * (1.0 / DEPTH))
             base = jnp.floor(wrapped)
@@ -406,30 +408,131 @@
             for color in range(3):
                 term = weight * jnp.tanh((0.5 * steep_s[color]) * (sample - mid_s[color]))
                 sums[color] = term if sums[color] is None else sums[color] + term
-        layers += [0.5 * ((1.0 - clear) + total) for total in sums]
-        layers.append(depth)
+        return clear, sums, depth
+
+    theta = {}
+
+    def finish(y, h, t):
+        head_v[pl.ds(y, SIDE, stride=SIDE), :] = h
+        temp_v[pl.ds(y, SIDE, stride=SIDE), :] = t
+        theta[y] = 0.05 + 0.4 * jnp.exp(0.8 * jnp.minimum(h, 0.0))
+
+    receive(x_waits)
+    x_ghost = [read_ghost(x_part, side, has_x[side]) for side in range(2)]
+    keep(0, x_ghost)
+    bases = [base_of(y, head, temp, conduct, 0) for y in range(SIDE)]
+    faces, head_1, temp_1, conduct_1 = {}, {}, {}, {}
+
+    def first_step(y):
+        head_1[y], temp_1[y] = plane_step(y, head, temp, conduct, bases[y], faces)
+        conduct_1[y] = conductivity(head_1[y], temp_1[y], ks[y], alpha[y], ice[y])
+
+    for y in range(1, SIDE - 1):
+        first_step(y)
+    x_bases = [
+        ghost_base(x_ghost[side], (edge[x][0], edge[x][1], edge[x][4]))
+        for side, x in ((0, 0), (1, SIDE - 1))
+    ]
+    nothing = jnp.zeros((1, DEPTH), F32)
+    keep(
+        2,
+        [
+            ghost_step(x_ghost[side], x_bases[side], ((nothing,) * 3,) * 2, y_open, has_x[side])
+            for side in range(2)
+        ],
+    )
+    bases_1 = {y: base_of(y, head_1, temp_1, conduct_1, 2) for y in range(1, SIDE - 1)}
+    faces_1 = {}
+    middle = range(2, SIDE - 2)
+    for y in middle:
+        finish(y, *plane_step(y, head_1, temp_1, conduct_1, bases_1[y], faces_1))
+    middles = [view_planes(view, middle, theta) for view in range(VIEWS)]
+
+    receive(y_waits)
+    y_ghost = [read_ghost(y_part, side, has_y[side]) for side in range(2)]
+    for side, y in ((0, -1), (1, SIDE)):
+        head[y], temp[y], conduct[y] = y_ghost[side][:3]
+    for y in (0, SIDE - 1):
+        first_step(y)
+    for side, y, out in ((0, 0, -1), (1, SIDE - 1, SIDE)):
+        head_1[out], temp_1[out], conduct_1[out] = ghost_step(
+            y_ghost[side],
+            ghost_base(y_ghost[side], (head[y], temp[y], conduct[y])),
+            (corner(0, side), corner(1, side)),
+            x_open,
+            has_y[side],
+        )
+    keep(
+        4,
+        [
+            ghost_step(
+                x_ghost[side],
+                x_bases[side],
+                (corner(side, 0), corner(side, 1)),
+                y_open,
+                has_x[side],
+            )
+            for side in range(2)
+        ],
+    )
+    for y in (0, SIDE - 1):
+        bases_1[y] = base_of(y, head_1, temp_1, conduct_1, 4)
+    for y in (0, 1, SIDE - 2, SIDE - 1):
+        finish(y, *plane_step(y, head_1, temp_1, conduct_1, bases_1[y], faces_1))
+
+    layers = []
+    for view in range(VIEWS):
+        clear_a, sums_a, depth_a = view_planes(view, (0, 1), theta)
+        clear_b, sums_b, depth_b = middles[view]
+        clear_c, sums_c, depth_c = view_planes(view, (SIDE - 2, SIDE - 1), theta)
+        opaque = 1.0 - clear_a * (clear_b * clear_c)
+        for color in range(3):
+            total = sums_a[color] + clear_a * (sums_b[color] + clear_b * sums_c[color])
+            layers.append(0.5 * (opaque + total))
+        layers.append(depth_a + depth_b + depth_c)
     piece_send[...] = jnp.transpose(jnp.concatenate(layers, 0))
 
     def exchange(src, dst, device):
         return pltpu.make_async_remote_copy(
             src_ref=src,
             dst_ref=dst,
-            send_sem=piece_send_sem,
+            send_sem=local_sem.at[8],
             recv_sem=piece_recv_sem,
             device_id=device,
             device_id_type=MESH,
         )
 
-    @pl.when(jnp.logical_not(is_hub))
-    def _():
-        pl.semaphore_wait(known_sem, 1)
-
-    for peer in peers:
+    plain = jnp.logical_not(jnp.logical_or(is_hub, is_late))
+
+    def give(peer):
         exchange(
             piece_send.at[pl.ds(pl.multiple_of(peer * SIDE, SIDE), SIDE)],
             piece_recv.at[gy],
             (gx, peer),
         ).start()
+
+    @pl.when(plain)
+    def _():
+        pl.semaphore_wait(known_sem.at[MOST], 1)
+
+    @pl.when(is_late)
+    def _():
+        pl.semaphore_wait(known_sem.at[ALL], 1)
+
+    for peer in peers:
+
+        @pl.when(peer != HUB - 1)
+        def _():
+            give(peer)
+
+    @pl.when(plain)
+    def _():
+        pl.semaphore_wait(known_sem.at[ALL], 1)
+
+    @pl.when(jnp.logical_not(is_late))
+    def _():
+        give(HUB - 1)
+
     piece_recv[gy] = piece_send[pl.ds(pl.multiple_of(gy * SIDE, SIDE), SIDE), :]
 
     view_of = lax.div(lane, 4 * SIDE)
@@ -445,7 +548,7 @@
     exchange_in = pltpu.make_async_remote_copy(
         src_ref=piece_recv.at[pl.ds(0, GROUPS - 1)],
         dst_ref=piece_recv.at[pl.ds(0, GROUPS - 1)],
-        send_sem=piece_send_sem,
+        send_sem=local_sem.at[8],
         recv_sem=piece_recv_sem,
         device_id=(gx, gy_lo),
         device_id_type=MESH,
@@ -466,7 +569,7 @@
     color = sum(jnp.exp(-fronts[group]) * piece_recv[group] for group in range(GROUPS))
     opaque = 1.0 - jnp.exp(-sum(depths))
     image_v[...] = jnp.transpose(jnp.where(is_depth, opaque, color))
-    for present, copy in waits:
+    for present, copy in x_waits + y_waits:
 
         @pl.when(present)
         def _():
@@ -517,15 +620,12 @@
             vmem((2, 7 * SIDE, DEPTH), F32),
             vmem((2, 2, 4, DEPTH), F32),
             vmem((2, 2, 4, DEPTH), F32),
-            vmem((4, 3, SIDE, DEPTH), F32),
+            vmem((6, 3, SIDE, DEPTH), F32),
             vmem((DEPTH, DEPTH), F32),
             vmem((GROUPS, SIDE, DEPTH), F32),
-            dma((4,)),
-            dma((6,)),
+            dma((10,)),
             dma((8,)),
-            dma((8,)),
-            pltpu.SemaphoreType.REGULAR(()),
-            dma(()),
+            pltpu.SemaphoreType.REGULAR((6,)),
             dma(()),
         ],
         compiler_params=pltpu.CompilerParams(collective_id=0, has_side_effects=True),

time: 23.7 us -> 22.5 us (0.949)
  Pallas kernels: 22.8 us -> 21.5 us
    pallas_call x1, Pallas kernels: 22.1 us -> 20.8 us  [shards(): pl.pallas_call(functools.partial(kernel, gx_count, gy_count), out_shape=t...]
where the time goes in v4:
time: 22.5 us; the launch traced here: 22.2 us
  Pallas kernels  21.5 us (96%)
  between operations  0.64 us (3%)
    pallas_call x1, Pallas kernels, shards(): pl.pallas_call(functools.partial(kernel, gx_count, gy_count), out_shape=t...  20.8 us
    pallas_call x1, Pallas kernels, shards(): pl.pallas_call(put_out, out_shape=tuple((jax.ShapeDtypeStruct(shape, F32)...  0.67 us

profile of v4, /device:TPU:1, one launch (start us, length us, event | category | flops | bytes accessed | tf_op | source)
XLA Modules:
  0.0 22.2 jit_solution(9973508203631558688)
XLA Ops:
  0.6 20.8 %step_and_view.1 = (f32[64,128]{1,0:T(8,128)S(1)}, f32[64,128]{1,0:T(8,128)S(1)}, f32[128,8]{1,0:T(8,128)S(1)}) custom-call(f32[64,128]{1,0:T(8,128)} %bitcast.7, f32[64,128]{1,0:T(8,128)} %bitcast.8, s32[64,128]{1,0:T(8,128)} %bitcast.9, s32[64,128]{1,0:T(8,128)} %bitcast.10, f32[12]{0:T(128)} %ks_in.1, f32[12]{0:T(128)} %alpha_in.1, f32[4]{0:T(128)} %skew_in.1, ...), custom_call_target="tpu_custom_call" | custom-call | tf_op jit(solution)/shard_map/step_and_view/pallas_call | solution.py:601
  21.5 0.7 %put_out.1 = (f32[64,128]{1,0:T(8,128)}, f32[64,128]{1,0:T(8,128)}, f32[128,8]{1,0:T(8,128)}) custom-call(f32[64,128]{1,0:T(8,128)S(1)} %get-tuple-element.9.head_v, f32[64,128]{1,0:T(8,128)S(1)} %get-tuple-element.10.temp_v, f32[128,8]{1,0:T(8,128)S(1)} %get-tuple-element.11.image_v), custom_call_target="tpu_custom_call" | custom-call | tf_op jit(solution)/shard_map/put_out/pallas_call | solution.py:634

commit v5 on v4

--- a/solution.py
+++ b/solution.py
@@ -15,6 +15,7 @@
 GROUPS = 16
 DIFFUSE = 0.12
 HUB = 1
+LATE = 2
 BEFORE, CROSS, BELOW, DIAGONAL, MOST, ALL = range(6)
 F32 = jnp.float32
 
@@ -31,12 +32,14 @@
 
 
 def vertical(head, temp, conduct, lane):
-    above = pltpu.roll(head, DEPTH - 1, 1)
-    conduct_above = pltpu.roll(conduct, DEPTH - 1, 1)
-    flux = jnp.where(lane < DEPTH - 1, (conduct + conduct_above) * (above - head + 1.0), 0.0)
-    change = flux - pltpu.roll(flux, 1, 1)
-    warm = jnp.where(lane < DEPTH - 1, pltpu.roll(temp, DEPTH - 1, 1), 0.0) + jnp.where(
-        lane > 0, pltpu.roll(temp, 1, 1), 0.0
+    inner_lo, inner_hi = lane > 0, lane < DEPTH - 1
+    above, conduct_above = (pltpu.roll(a, DEPTH - 1, 1) for a in (head, conduct))
+    below, conduct_below = (pltpu.roll(a, 1, 1) for a in (head, conduct))
+    change = jnp.where(inner_hi, (conduct + conduct_above) * (above - head + 1.0), 0.0) - jnp.where(
+        inner_lo, (conduct + conduct_below) * (head - below + 1.0), 0.0
+    )
+    warm = jnp.where(inner_hi, pltpu.roll(temp, DEPTH - 1, 1), 0.0) + jnp.where(
+        inner_lo, pltpu.roll(temp, 1, 1), 0.0
     )
     return change, warm
 
@@ -185,7 +188,7 @@
     lane = lax.broadcasted_iota(jnp.int32, (SIDE, DEPTH), 1)
     first, last = row == 0, row == SIDE - 1
 
-    for copy in params + loads:
+    for copy in params[:2] + loads:
         copy.wait()
 
     def across(ref, y):
@@ -234,7 +237,7 @@
         return pltpu.make_async_remote_copy(
             src_ref=src,
             dst_ref=dst,
-            send_sem=local_sem.at[mine],
+            send_sem=local_sem.at[(0, 1, 2, 3, 4, 5, 10, 11)[mine]],
             recv_sem=halo_recv_sem.at[theirs],
             device_id=device,
             device_id_type=MESH,
@@ -273,6 +276,9 @@
             tell(ALL, (gx, peer))
 
     send(both[0][0], c_copy(0, 0), DIAGONAL)
+
+    for copy in params[2:]:
+        copy.wait()
 
     x_open = (jnp.logical_or(row > 0, has_x[0]), jnp.logical_or(row < SIDE - 1, has_x[1]))
     y_open = (jnp.logical_or(row > 0, has_y[0]), jnp.logical_or(row < SIDE - 1, has_y[1]))
@@ -397,7 +403,7 @@
             part = wrapped - base
             turn = lax.rem(2 * DEPTH - base.astype(jnp.int32), DEPTH)
             lower = pltpu.roll(theta[y], turn, 1)
-            upper = pltpu.roll(lower, DEPTH - 1, 1)
+            upper = pltpu.roll(theta[y], lax.rem(turn + DEPTH - 1, DEPTH), 1)
             sample = (1.0 - part) * lower + part * upper
             optical = sample * (8.0 / planes_all)
             passed = jnp.exp(-optical)
@@ -492,12 +498,14 @@
         layers.append(depth_a + depth_b + depth_c)
     piece_send[...] = jnp.transpose(jnp.concatenate(layers, 0))
 
+    among_late = jnp.where(gy < LATE, 1, 0)
+
     def exchange(src, dst, device):
         return pltpu.make_async_remote_copy(
             src_ref=src,
             dst_ref=dst,
-            send_sem=local_sem.at[8],
-            recv_sem=piece_recv_sem,
+            send_sem=local_sem.at[6],
+            recv_sem=piece_recv_sem.at[among_late],
             device_id=device,
             device_id_type=MESH,
         )
@@ -545,29 +553,45 @@
         ranks.append(rank)
     is_depth = kind_of == 3
 
-    exchange_in = pltpu.make_async_remote_copy(
-        src_ref=piece_recv.at[pl.ds(0, GROUPS - 1)],
-        dst_ref=piece_recv.at[pl.ds(0, GROUPS - 1)],
-        send_sem=local_sem.at[8],
-        recv_sem=piece_recv_sem,
-        device_id=(gx, gy_lo),
-        device_id_type=MESH,
-    )
-    exchange_in.wait_recv()
-
-    depths = []
-    for group in range(GROUPS):
+    def arrive(number, tiles):
+        slots = piece_recv.at[pl.ds(0, tiles)]
+        pltpu.make_async_remote_copy(
+            src_ref=slots,
+            dst_ref=slots,
+            send_sem=local_sem.at[6],
+            recv_sem=piece_recv_sem.at[number],
+            device_id=(gx, gy_lo),
+            device_id_type=MESH,
+        ).wait_recv()
+
+    depths, fronts = {}, {}
+
+    def place(group):
         value = jnp.where(is_depth, piece_recv[group], 0.0)
         value = value + pltpu.roll(value, DEPTH - SIDE, 1)
-        depths.append(value + pltpu.roll(value, DEPTH - 2 * SIDE, 1))
-    fronts = [jnp.zeros((SIDE, DEPTH), F32)] * GROUPS
-    for one in range(GROUPS):
-        for two in range(one + 1, GROUPS):
-            before = ranks[two] < ranks[one]
-            fronts[one] = fronts[one] + jnp.where(before, depths[two], 0.0)
-            fronts[two] = fronts[two] + jnp.where(before, 0.0, depths[one])
+        depths[group] = value + pltpu.roll(value, DEPTH - 2 * SIDE, 1)
+        total = jnp.zeros((SIDE, DEPTH), F32)
+        for other in fronts:
+            before = ranks[other] < ranks[group]
+            total = total + jnp.where(before, depths[other], 0.0)
+            fronts[other] = fronts[other] + jnp.where(before, 0.0, depths[group])
+        fronts[group] = total
+
+    for number, groups, tiles in ((0, range(LATE, GROUPS), GROUPS - LATE), (1, range(LATE), LATE)):
+        own_late = among_late == number
+
+        @pl.when(own_late)
+        def _():
+            arrive(number, tiles - 1)
+
+        @pl.when(jnp.logical_not(own_late))
+        def _():
+            arrive(number, tiles)
+
+        for group in groups:
+            place(group)
     color = sum(jnp.exp(-fronts[group]) * piece_recv[group] for group in range(GROUPS))
-    opaque = 1.0 - jnp.exp(-sum(depths))
+    opaque = 1.0 - jnp.exp(-sum(depths.values()))
     image_v[...] = jnp.transpose(jnp.where(is_depth, opaque, color))
     for present, copy in x_waits + y_waits:
 
@@ -575,7 +599,15 @@
         def _():
             copy.wait_send()
 
-    exchange_in.wait_send()
+    sent = piece_recv.at[pl.ds(0, GROUPS - 1)]
+    pltpu.make_async_remote_copy(
+        src_ref=sent,
+        dst_ref=sent,
+        send_sem=local_sem.at[6],
+        recv_sem=piece_recv_sem.at[0],
+        device_id=(gx, gy_lo),
+        device_id_type=MESH,
+    ).wait_send()
 
 
 def put_out(head_v, temp_v, image_v, head_out, temp_out, image_out, sem):
@@ -623,10 +655,10 @@
             vmem((6, 3, SIDE, DEPTH), F32),
             vmem((DEPTH, DEPTH), F32),
             vmem((GROUPS, SIDE, DEPTH), F32),
-            dma((10,)),
+            dma((12,)),
             dma((8,)),
             pltpu.SemaphoreType.REGULAR((6,)),
-            dma(()),
+            dma((2,)),
         ],
         compiler_params=pltpu.CompilerParams(collective_id=0, has_side_effects=True),
         name="step_and_view",

time: 22.5 us -> 22.3 us (level)
    pallas_call x1, Pallas kernels: 20.8 us -> 20.6 us  [shards(): pl.pallas_call(functools.partial(kernel, gx_count, gy_count), out_shape=t...]
where the time goes in v5:
time: 22.3 us; the launch traced here: 21.9 us
  Pallas kernels  21.3 us (96%)
  between operations  0.64 us (3%)
    pallas_call x1, Pallas kernels, shards(): pl.pallas_call(functools.partial(kernel, gx_count, gy_count), out_shape=t...  20.6 us
    pallas_call x1, Pallas kernels, shards(): pl.pallas_call(put_out, out_shape=tuple((jax.ShapeDtypeStruct(shape, F32)...  0.67 us

profile of v5, /device:TPU:1, one launch (start us, length us, event | category | flops | bytes accessed | tf_op | source)
XLA Modules:
  0.0 21.9 jit_solution(10544564079440733688)
XLA Ops:
  0.6 20.6 %step_and_view.1 = (f32[64,128]{1,0:T(8,128)S(1)}, f32[64,128]{1,0:T(8,128)S(1)}, f32[128,8]{1,0:T(8,128)S(1)}) custom-call(f32[64,128]{1,0:T(8,128)} %bitcast.7, f32[64,128]{1,0:T(8,128)} %bitcast.8, s32[64,128]{1,0:T(8,128)} %bitcast.9, s32[64,128]{1,0:T(8,128)} %bitcast.10, f32[12]{0:T(128)} %ks_in.1, f32[12]{0:T(128)} %alpha_in.1, f32[4]{0:T(128)} %skew_in.1, ...), custom_call_target="tpu_custom_call" | custom-call | tf_op jit(solution)/shard_map/step_and_view/pallas_call | solution.py:633
  21.3 0.7 %put_out.1 = (f32[64,128]{1,0:T(8,128)}, f32[64,128]{1,0:T(8,128)}, f32[128,8]{1,0:T(8,128)}) custom-call(f32[64,128]{1,0:T(8,128)S(1)} %get-tuple-element.9.head_v, f32[64,128]{1,0:T(8,128)S(1)} %get-tuple-element.10.temp_v, f32[128,8]{1,0:T(8,128)S(1)} %get-tuple-element.11.image_v), custom_call_target="tpu_custom_call" | custom-call | tf_op jit(solution)/shard_map/put_out/pallas_call | solution.py:666

commit v6 on v5

--- a/solution.py
+++ b/solution.py
@@ -29,6 +29,10 @@
 
 def conductivity(head, temp, ks, alpha, ice):
     return ks * jnp.exp(alpha * jnp.minimum(head, 0.0) + 2.0 * ice * (jnp.tanh(temp) - 1.0))
+
+
+def face(k_a, h_a, k_b, h_b):
+    return (k_a + k_b) * (h_b - h_a)
 
 
 def vertical(head, temp, conduct, lane):
@@ -205,34 +209,6 @@
         ks[y], alpha[y] = lookup(category[y], ks_s), lookup(category[y], alpha_s)
         conduct[y] = conductivity(head[y], temp[y], ks[y], alpha[y], ice[y])
 
-    for y in (0, 1, SIDE - 2, SIDE - 1):
-        own(y)
-    edge = {}
-    for x in (0, 1, SIDE - 2, SIDE - 1):
-        h, t, c = tile(head_a, x), tile(temp_a, x), tile(cat_a, x)
-        i = tile(ice_a, x).astype(F32)
-        k = conductivity(h, t, lookup(c, ks_s), lookup(c, alpha_s), i)
-        edge[x] = (h, t, c.astype(F32), i, k)
-
-    for side, (near, far) in enumerate(((0, 1), (SIDE - 1, SIDE - 2))):
-        parts = (
-            head[near],
-            temp[near],
-            category[near].astype(F32),
-            ice[near],
-            head[far],
-            temp[far],
-            conduct[far],
-        )
-        for number, part in enumerate(parts):
-            y_send[side, pl.ds(number * SIDE, SIDE), :] = part
-        parts = (*edge[near][:4], edge[far][0], edge[far][1], edge[far][4])
-        for number, part in enumerate(parts):
-            x_send[side, pl.ds(number * SIDE, SIDE), :] = part
-    for number, (x, y) in enumerate(((0, 0), (0, 7), (7, 0), (7, 7))):
-        for field, part in enumerate((head[y], temp[y], conduct[y], conduct[y])):
-            c_send[number // 2, number % 2, pl.ds(field, 1), :] = part[x : x + 1, :]
-
     def remote(src, dst, mine, theirs, device):
         return pltpu.make_async_remote_copy(
             src_ref=src,
@@ -262,10 +238,42 @@
                 pl.semaphore_wait(known_sem.at[number], 1)
             copy.start()
 
+    def stage_y(side):
+        near, far = ((0, 1), (SIDE - 1, SIDE - 2))[side]
+        own(near)
+        own(far)
+        parts = (
+            head[near],
+            temp[near],
+            category[near].astype(F32),
+            ice[near],
+            face(conduct[near], head[near], conduct[far], head[far]),
+            temp[far],
+        )
+        for number, part in enumerate(parts):
+            y_send[side, pl.ds(number * SIDE, SIDE), :] = part
+        for a, x in enumerate((0, SIDE - 1)):
+            for field, part in enumerate((head[near], temp[near], conduct[near], conduct[near])):
+                c_send[a, side, pl.ds(field, 1), :] = part[x : x + 1, :]
+
+    stage_y(1)
     for a in range(2):
         send(both[a][1], c_copy(a, 1))
     send(has_y[1], y_copy(1))
+
+    edge = {}
+    for x in (0, 1, SIDE - 2, SIDE - 1):
+        h, t, c = tile(head_a, x), tile(temp_a, x), tile(cat_a, x)
+        i = tile(ice_a, x).astype(F32)
+        k = conductivity(h, t, lookup(c, ks_s), lookup(c, alpha_s), i)
+        edge[x] = (h, t, c.astype(F32), i, k)
+    for side, (near, far) in enumerate(((0, 1), (SIDE - 1, SIDE - 2))):
+        inner, outer = edge[far], edge[near]
+        parts = (*outer[:4], face(outer[4], outer[0], inner[4], inner[0]), inner[1])
+        for number, part in enumerate(parts):
+            x_send[side, pl.ds(number * SIDE, SIDE), :] = part
     send(has_x[1], x_copy(1))
+    stage_y(0)
     send(has_x[0], x_copy(0), BEFORE)
     send(both[1][0], c_copy(1, 0), CROSS)
     send(has_y[0], y_copy(0), BELOW)
@@ -342,19 +350,16 @@
     def read_ghost(part_of, side, present):
         h, t, c, i = (part_of(side, number) for number in range(4))
         k_s, a = lookup(c, ks_s), lookup(c, alpha_s)
-        far = tuple(part_of(side, number) for number in range(4, 7))
+        far = tuple(part_of(side, number) for number in range(4, 6))
         return h, warm_if(present, t), conductivity(h, t, k_s, a, i), k_s, a, i, far
 
     def step(h, t, change, warm):
         return h + 0.5 * change, t + DIFFUSE * (warm - 6.0 * t)
-
-    def face(k_a, h_a, k_b, h_b):
-        return (k_a + k_b) * (h_b - h_a)
 
     def ghost_base(cell, inner):
         h, t, k, far = cell[0], cell[1], cell[2], cell[6]
         change, warm = vertical(h, t, k, lane)
-        change = change + face(k, h, far[2], far[0]) + face(k, h, inner[2], inner[0])
+        change = change + far[0] + face(k, h, inner[2], inner[0])
         return change, warm + far[1] + inner[1]
 
     def ghost_step(cell, base, ends, opened, present):
@@ -646,10 +651,10 @@
             pltpu.SMEM((3,), F32),
             pltpu.SMEM((3,), F32),
             pltpu.SMEM((VIEWS, GROUPS), jnp.int32),
-            vmem((2, 7 * SIDE, DEPTH), F32),
-            vmem((2, 7 * SIDE, DEPTH), F32),
-            vmem((2, 7 * SIDE, DEPTH), F32),
-            vmem((2, 7 * SIDE, DEPTH), F32),
+            vmem((2, 6 * SIDE, DEPTH), F32),
+            vmem((2, 6 * SIDE, DEPTH), F32),
+            vmem((2, 6 * SIDE, DEPTH), F32),
+            vmem((2, 6 * SIDE, DEPTH), F32),
             vmem((2, 2, 4, DEPTH), F32),
             vmem((2, 2, 4, DEPTH), F32),
             vmem((6, 3, SIDE, DEPTH), F32),

time: 22.3 us -> 22.2 us (level)
  no operation moved by 1% of the time
where the time goes in v6:
time: 22.2 us; the launch traced here: 21.9 us
  Pallas kernels  21.3 us (96%)
  between operations  0.64 us (3%)
    pallas_call x1, Pallas kernels, shards(): pl.pallas_call(functools.partial(kernel, gx_count, gy_count), out_shape=t...  20.6 us
    pallas_call x1, Pallas kernels, shards(): pl.pallas_call(put_out, out_shape=tuple((jax.ShapeDtypeStruct(shape, F32)...  0.67 us

profile of v6, /device:TPU:1, one launch (start us, length us, event | category | flops | bytes accessed | tf_op | source)
XLA Modules:
  0.0 21.9 jit_solution(5789881180128978913)
XLA Ops:
  0.6 20.6 %step_and_view.1 = (f32[64,128]{1,0:T(8,128)S(1)}, f32[64,128]{1,0:T(8,128)S(1)}, f32[128,8]{1,0:T(8,128)S(1)}) custom-call(f32[64,128]{1,0:T(8,128)} %bitcast.7, f32[64,128]{1,0:T(8,128)} %bitcast.8, s32[64,128]{1,0:T(8,128)} %bitcast.9, s32[64,128]{1,0:T(8,128)} %bitcast.10, f32[12]{0:T(128)} %ks_in.1, f32[12]{0:T(128)} %alpha_in.1, f32[4]{0:T(128)} %skew_in.1, ...), custom_call_target="tpu_custom_call" | custom-call | tf_op jit(solution)/shard_map/step_and_view/pallas_call | solution.py:638
  21.2 0.7 %put_out.1 = (f32[64,128]{1,0:T(8,128)}, f32[64,128]{1,0:T(8,128)}, f32[128,8]{1,0:T(8,128)}) custom-call(f32[64,128]{1,0:T(8,128)S(1)} %get-tuple-element.9.head_v, f32[64,128]{1,0:T(8,128)S(1)} %get-tuple-element.10.temp_v, f32[128,8]{1,0:T(8,128)S(1)} %get-tuple-element.11.image_v), custom_call_target="tpu_custom_call" | custom-call | tf_op jit(solution)/shard_map/put_out/pallas_call | solution.py:671

commit v7 on v6

--- a/solution.py
+++ b/solution.py
@@ -532,7 +532,13 @@
     def _():
         pl.semaphore_wait(known_sem.at[ALL], 1)
 
-    for peer in peers:
+    @pl.when(is_hub)
+    def _():
+        give(HUB - 1)
+
+    soon = [(2, 3), (1, 3), (3, 3), (2, 0), (1, 0), (3, 0)]
+    for dx, dy in soon + [d for d in shifts if d not in soon]:
+        peer = lax.rem(px + dx, 4) * 4 + lax.rem(py + dy, 4)
 
         @pl.when(peer != HUB - 1)
         def _():
@@ -541,9 +547,6 @@
     @pl.when(plain)
     def _():
         pl.semaphore_wait(known_sem.at[ALL], 1)
-
-    @pl.when(jnp.logical_not(is_late))
-    def _():
         give(HUB - 1)
 
     piece_recv[gy] = piece_send[pl.ds(pl.multiple_of(gy * SIDE, SIDE), SIDE), :]

time: 22.2 us -> 22.1 us (level)
  no operation moved by 1% of the time
where the time goes in v7:
time: 22.1 us; the launch traced here: 21.8 us
  Pallas kernels  21.2 us (96%)
  between operations  0.64 us (3%)
    pallas_call x1, Pallas kernels, shards(): pl.pallas_call(functools.partial(kernel, gx_count, gy_count), out_shape=t...  20.5 us
    pallas_call x1, Pallas kernels, shards(): pl.pallas_call(put_out, out_shape=tuple((jax.ShapeDtypeStruct(shape, F32)...  0.67 us

profile of v7, /device:TPU:1, one launch (start us, length us, event | category | flops | bytes accessed | tf_op | source)
XLA Modules:
  0.0 21.8 jit_solution(6191794968252385861)
XLA Ops:
  0.6 20.5 %step_and_view.1 = (f32[64,128]{1,0:T(8,128)S(1)}, f32[64,128]{1,0:T(8,128)S(1)}, f32[128,8]{1,0:T(8,128)S(1)}) custom-call(f32[64,128]{1,0:T(8,128)} %bitcast.7, f32[64,128]{1,0:T(8,128)} %bitcast.8, s32[64,128]{1,0:T(8,128)} %bitcast.9, s32[64,128]{1,0:T(8,128)} %bitcast.10, f32[12]{0:T(128)} %ks_in.1, f32[12]{0:T(128)} %alpha_in.1, f32[4]{0:T(128)} %skew_in.1, ...), custom_call_target="tpu_custom_call" | custom-call | tf_op jit(solution)/shard_map/step_and_view/pallas_call | solution.py:641
  21.1 0.7 %put_out.1 = (f32[64,128]{1,0:T(8,128)}, f32[64,128]{1,0:T(8,128)}, f32[128,8]{1,0:T(8,128)}) custom-call(f32[64,128]{1,0:T(8,128)S(1)} %get-tuple-element.9.head_v, f32[64,128]{1,0:T(8,128)S(1)} %get-tuple-element.10.temp_v, f32[128,8]{1,0:T(8,128)S(1)} %get-tuple-element.11.image_v), custom_call_target="tpu_custom_call" | custom-call | tf_op jit(solution)/shard_map/put_out/pallas_call | solution.py:674

commit v8 on v7

--- a/solution.py
+++ b/solution.py
@@ -21,10 +21,14 @@
 
 
 def lookup(category, table):
-    total = jnp.full(category.shape, table[0], F32)
-    for number in range(1, SOILS):
-        total = jnp.where(category == number, table[number], total)
-    return total
+    half = SOILS // 2
+    parts = []
+    for start in (0, half):
+        total = jnp.full(category.shape, table[start], F32)
+        for number in range(start + 1, start + half):
+            total = jnp.where(category == number, table[number], total)
+        parts.append(total)
+    return jnp.where(category < half, *parts)
 
 
 def conductivity(head, temp, ks, alpha, ice):

time: 22.1 us -> 22.1 us (level)
  no operation moved by 1% of the time
where the time goes in v8:
time: 22.1 us; the launch traced here: 21.8 us
  Pallas kernels  21.1 us (95%)
  between operations  0.64 us (3%)
    pallas_call x1, Pallas kernels, shards(): pl.pallas_call(functools.partial(kernel, gx_count, gy_count), out_shape=t...  20.5 us
    pallas_call x1, Pallas kernels, shards(): pl.pallas_call(put_out, out_shape=tuple((jax.ShapeDtypeStruct(shape, F32)...  0.67 us

profile of v8, /device:TPU:1, one launch (start us, length us, event | category | flops | bytes accessed | tf_op | source)
XLA Modules:
  0.0 21.8 jit_solution(6997140121452104866)
XLA Ops:
  0.6 20.5 %step_and_view.1 = (f32[64,128]{1,0:T(8,128)S(1)}, f32[64,128]{1,0:T(8,128)S(1)}, f32[128,8]{1,0:T(8,128)S(1)}) custom-call(f32[64,128]{1,0:T(8,128)} %bitcast.7, f32[64,128]{1,0:T(8,128)} %bitcast.8, s32[64,128]{1,0:T(8,128)} %bitcast.9, s32[64,128]{1,0:T(8,128)} %bitcast.10, f32[12]{0:T(128)} %ks_in.1, f32[12]{0:T(128)} %alpha_in.1, f32[4]{0:T(128)} %skew_in.1, ...), custom_call_target="tpu_custom_call" | custom-call | tf_op jit(solution)/shard_map/step_and_view/pallas_call | solution.py:645
  21.1 0.7 %put_out.1 = (f32[64,128]{1,0:T(8,128)}, f32[64,128]{1,0:T(8,128)}, f32[128,8]{1,0:T(8,128)}) custom-call(f32[64,128]{1,0:T(8,128)S(1)} %get-tuple-element.9.head_v, f32[64,128]{1,0:T(8,128)S(1)} %get-tuple-element.10.temp_v, f32[128,8]{1,0:T(8,128)S(1)} %get-tuple-element.11.image_v), custom_call_target="tpu_custom_call" | custom-call | tf_op jit(solution)/shard_map/put_out/pallas_call | solution.py:678
